TPU v7x, 512 devices: a whole 4x8x8 slice. The times are simulated.
512 devices in a mesh: dp: 32 (over z_lo, y, core), expert: 16 (over x, z_hi).
Axes of the slice: x: 4, y: 8, z: 8 (z_hi: 4, z_lo: 2; z = z_hi * 2 + z_lo), core: 2. Of those that a mesh axis runs over, the one named last changes fastest.
Arguments:
- grad_out: bfloat16 [4, 32768, 1024], P(None, ('dp', 'expert')), may hold values from -12 to 12
- routes: int32 [4, 32768, 8], P(None, ('dp', 'expert')), may hold values from 0 to 127, all different within a row; in each aligned block of 64 rows (0 to 63, 64 to 127, ..., all dimensions but the last counted through in order) at most 8 rows name the same one
- route_probs: bfloat16 [4, 32768, 8], P(None, ('dp', 'expert')), may hold values from 0.049804688 to 0.3984375
- dispatched: bfloat16 [4, 65536, 1024], P(None, ('dp', 'expert')), may hold values from -12 to 12, as said below
- w_gate: bfloat16 [1024, 4096], P(None, 'expert'), may hold values from -0.1875 to 0.1875
- w_up: bfloat16 [1024, 4096], P(None, 'expert'), may hold values from -0.1875 to 0.1875
- w_down: bfloat16 [4096, 1024], P('expert'), may hold values from -0.25 to 0.25
Outputs:
- grad_in: bfloat16 [4, 32768, 1024], P(None, ('dp', 'expert'))
- grad_gate: float32 [1024, 4096], P('dp', 'expert')
- grad_up: float32 [1024, 4096], P('dp', 'expert')
- grad_down_t: float32 [1024, 4096], P('dp', 'expert')
Inputs may be any that keep to these rules, and one draw needn't show every extreme that they name: `routes`: in each micro-batch, among the 64 rows of one device no expert is named more than 8 times, a bound that some expert reaches in some of these blocks. `dispatched`: within each group of 16 consecutive blocks of 128 rows, blocks 2e and 2e + 1 are equal.
All inputs are finite; a program needn't handle non-finite values.
Results may differ from a plain program's by a relative error of at most 0.0058.
Values may be sent and summed in bfloat16 or wider, within the bound.
No kernel may reach another device: no remote copies, remote signals or barrier semaphores. Data moves between devices by JAX's collectives and lax.ppermute only.
A program may use at most 64 MiB of HBM per device.

v0:
```python
import jax
import jax.numpy as jnp
from jax import lax
from jax.sharding import PartitionSpec as P

TOPK = 8
CAPS = 8


def swapped(x, axis, stride):
    return lax.ppermute(x, axis, [(i, i ^ 1 << stride) for i in range(lax.axis_size(axis))])


def in_one_piece(arrays, axis, dim, along):
    widths = [a.shape[along] for a in arrays]
    both = jnp.concatenate(arrays, axis=along)
    filled = lax.psum_scatter(both, axis, scatter_dimension=dim, tiled=True)
    return tuple(jnp.split(filled, [sum(widths[:k]) for k in range(1, len(widths))], axis=along))


def slot_take(route_ids, targets, flat_dy, flat_probs, capacity):
    hitting = (route_ids == targets[:, None]).astype(jnp.int32)
    ranking = jnp.cumsum(hitting, axis=1) - 1
    chosen = hitting[:, None, :] * (
        ranking[:, None, :] == jnp.arange(capacity, dtype=jnp.int32)[None, :, None]
    ).astype(jnp.int32)
    position = jnp.sum(
        chosen * jnp.arange(route_ids.shape[1], dtype=jnp.int32)[None, None, :], axis=2
    )
    living = jnp.sum(chosen, axis=2) > 0
    weights = jnp.take_along_axis(flat_probs, position, axis=1)
    rows_at = position // TOPK
    picked = jnp.take(flat_dy, rows_at.reshape(-1), axis=0)
    scaled = (weights.reshape(-1, 1).astype(jnp.float32) * picked.astype(jnp.float32)).astype(
        jnp.bfloat16
    )
    return jnp.where(living.reshape(-1, 1), scaled, jnp.zeros_like(scaled))


def contract_rows(left, right):
    return lax.dot_general(
        left, right, (((0,), (0,)), ((), ())), preferred_element_type=jnp.float32
    )


def contract_cols(left, right):
    return lax.dot_general(
        left, right, (((1,), (1,)), ((), ())), preferred_element_type=jnp.float32
    )


def per_device(grad_out, routes, route_probs, dispatched, w_gate, w_up, w_down):
    groups = lax.axis_size("expert")
    member = lax.axis_index("expert")
    window = groups // 2
    tok_dev = grad_out.shape[1]
    model_width = grad_out.shape[2]
    half_cols = w_gate.shape[1]
    capacity = CAPS
    half_caps = capacity // 2
    slot_count = groups * capacity
    parity = member % 2
    acc_gate = jnp.zeros((model_width, half_cols), jnp.float32)
    acc_up = jnp.zeros((model_width, half_cols), jnp.float32)
    acc_down = jnp.zeros((model_width, half_cols), jnp.float32)
    outputs = []
    for micro_idx in range(grad_out.shape[0]):
        own_ids = routes[micro_idx]
        targets = jnp.arange(window, dtype=jnp.int32)
        flat_ids = jnp.broadcast_to(own_ids.reshape(1, -1), (window, tok_dev * TOPK))
        flat_probs = jnp.broadcast_to(
            route_probs[micro_idx].reshape(1, -1), (window, tok_dev * TOPK)
        )
        sending = slot_take(flat_ids, targets, grad_out[micro_idx], flat_probs, capacity)
        arrived = lax.all_to_all(
            sending.reshape(groups, half_caps, model_width),
            "expert",
            split_axis=0,
            concat_axis=0,
            tiled=True,
        )
        partner_rows = swapped(arrived, "expert", 0)
        lower = jnp.where(parity == 0, arrived, partner_rows)
        upper = jnp.where(parity == 0, partner_rows, arrived)
        scaled = jnp.concatenate([lower, upper], axis=1).reshape(slot_count, model_width)
        inputs = dispatched[micro_idx]
        gate_pre = jnp.dot(inputs, w_gate, preferred_element_type=jnp.float32)
        up_pre = jnp.dot(inputs, w_up, preferred_element_type=jnp.float32)
        sigmoid = jax.nn.sigmoid(gate_pre)
        activated = gate_pre * sigmoid
        hidden = (activated * up_pre).astype(jnp.bfloat16)
        acc_down = acc_down + contract_rows(scaled, hidden)
        dhidden = contract_cols(scaled, w_down)
        d_gate = (dhidden * up_pre * sigmoid * (1.0 + gate_pre * (1.0 - sigmoid))).astype(
            jnp.bfloat16
        )
        d_up = (dhidden * activated).astype(jnp.bfloat16)
        acc_gate = acc_gate + contract_rows(inputs, d_gate)
        acc_up = acc_up + contract_rows(inputs, d_up)
        partial_value = contract_cols(d_gate, w_gate) + contract_cols(d_up, w_up)
        blocks = partial_value.reshape(groups, half_caps, 2, model_width)
        kept_part = lax.dynamic_index_in_dim(blocks, parity, 2, keepdims=False)
        given_part = lax.dynamic_index_in_dim(blocks, 1 - parity, 2, keepdims=False)
        partner = swapped(given_part, "expert", 0)
        returned = lax.all_to_all(
            kept_part + partner, "expert", split_axis=0, concat_axis=0, tiled=True
        )
        summed = jnp.swapaxes(returned.reshape(window, 2, half_caps, model_width), 1, 2).reshape(
            window, capacity, model_width
        )
        inside = own_ids < window
        hitting = (
            own_ids.reshape(-1)[:, None] == jnp.arange(window, dtype=jnp.int32)[None, :]
        ).astype(jnp.int32)
        ranking = jnp.sum((jnp.cumsum(hitting, axis=0) - 1) * hitting, axis=1).reshape(
            tok_dev, TOPK
        )
        slot_keys = jnp.where(inside, own_ids * capacity + ranking, -1)
        mixing = jnp.sum(
            (
                slot_keys[:, :, None]
                == jnp.arange(window * capacity, dtype=jnp.int32)[None, None, :]
            ).astype(jnp.float32),
            axis=1,
        )
        grad_tokens = jnp.dot(
            mixing,
            summed.reshape(window * capacity, model_width),
            precision=lax.Precision.HIGHEST,
            preferred_element_type=jnp.float32,
        )
        outputs.append(grad_tokens.astype(jnp.bfloat16))
    reduced = in_one_piece((acc_gate, acc_up, acc_down), "dp", 0, 1)
    factor = 1.0 / (grad_out.shape[0] * lax.axis_size("dp"))
    return (jnp.stack(outputs), reduced[0] * factor, reduced[1] * factor, reduced[2] * factor)


def solution(mesh):
    return jax.shard_map(
        per_device,
        mesh=mesh,
        in_specs=(
            P(None, ("dp", "expert"), None),
            P(None, ("dp", "expert"), None),
            P(None, ("dp", "expert"), None),
            P(None, ("dp", "expert"), None),
            P(None, "expert"),
            P(None, "expert"),
            P("expert", None),
        ),
        out_specs=(
            P(None, ("dp", "expert"), None),
            P("dp", "expert"),
            P("dp", "expert"),
            P("dp", "expert"),
        ),
        check_vma=False,
    )
```

profile of v0, /device:TPU:4, one launch (start us, length us, event | category | flops | bytes accessed | tf_op | source)
XLA Modules:
  0.0 256.2 jit_solution(15513255890719942221)
XLA Ops:
  7.2 0.8 fusion.106
  8.9 1.1 reduce-window.50
  11.4 0.7 fusion.107
  12.4 1.1 reduce-window.48
  15.1 0.9 gather_fusion.2
  16.2 0.7 gather_fusion.3
  17.0 0.7 reshape.509
  17.7 13.3 %all-to-all-start.2 = ((bf16[16,4,1024]{2,1,0:T(4,128)(2,1)}), bf16[16,4,1024]{2,1,0:T(4,128)(2,1)S(1)}, u32[]{:S(2)}, u32[]{:S(2)}) async-start(bf16[16,4,1024]{2,1,0:T(4,128)(2,1)} %reshape.509), calls=%async_computation.2 | async-start | bytes 262144 | tf_op jit(solution)/shard_map/all_to_all | solution.py:75
  31.3 1.1 reduce-window.52
  33.6 1.1 reduce-window.54
  37.8 0.9 gather_fusion
  39.1 0.9 gather_fusion.4
  40.4 0.9 gather_fusion.6
  41.5 0.7 gather_fusion.1
  42.3 0.7 reshape.503
  43.0 0.7 gather_fusion.7
  43.8 0.7 reshape.521
  44.5 0.7 gather_fusion.5
  45.4 0.7 reshape.515
  46.3 9.6 %all-to-all-start.6 = ((bf16[16,4,1024]{2,1,0:T(4,128)(2,1)}), bf16[16,4,1024]{2,1,0:T(4,128)(2,1)S(1)}, u32[]{:S(2)}, u32[]{:S(2)}) async-start(bf16[16,4,1024]{2,1,0:T(4,128)(2,1)} %reshape.521), calls=%async_computation.6 | async-start | bytes 262144 | tf_op jit(solution)/shard_map/all_to_all | solution.py:75
  56.2 8.2 %all-to-all-done.6 = bf16[16,4,1024]{2,1,0:T(4,128)(2,1)S(1)} async-done(((bf16[16,4,1024]{2,1,0:T(4,128)(2,1)}), bf16[16,4,1024]{2,1,0:T(4,128)(2,1)S(1)}, u32[]{:S(2)}, u32[]{:S(2)}) %all-to-all-start.6) | async-done | bytes 131104 | tf_op jit(solution)/shard_map/all_to_all | solution.py:75
  64.4 6.0 %all-to-all-start.4 = ((bf16[16,4,1024]{2,1,0:T(4,128)(2,1)}), bf16[16,4,1024]{2,1,0:T(4,128)(2,1)S(1)}, u32[]{:S(2)}, u32[]{:S(2)}) async-start(bf16[16,4,1024]{2,1,0:T(4,128)(2,1)} %reshape.515), calls=%async_computation.4 | async-start | bytes 262144 | tf_op jit(solution)/shard_map/all_to_all | solution.py:75
  70.6 4.3 %collective-permute-start.2 = (bf16[16,4,1024]{2,1,0:T(4,128)(2,1)S(1)}, bf16[16,4,1024]{2,1,0:T(4,128)(2,1)}, u32[]{:S(2)}, u32[]{:S(2)}) collective-permute-start(bf16[16,4,1024]{2,1,0:T(4,128)(2,1)S(1)} %all-to-all-done.2), channel_id=1, source_target_pairs={{0,1},{1,0},{2,3},{3,2},{4,5},{5,4},{6,7},{7,6},{8,9},{9,8},{10,11... | collective-permute-start | bytes 393224 | tf_op jit(solution)/shard_map/ppermute | solution.py:11
  74.9 4.4 %all-to-all-done.4 = bf16[16,4,1024]{2,1,0:T(4,128)(2,1)S(1)} async-done(((bf16[16,4,1024]{2,1,0:T(4,128)(2,1)}), bf16[16,4,1024]{2,1,0:T(4,128)(2,1)S(1)}, u32[]{:S(2)}, u32[]{:S(2)}) %all-to-all-start.4) | async-done | bytes 131104 | tf_op jit(solution)/shard_map/all_to_all | solution.py:75
  79.4 6.7 %all-to-all-start = ((bf16[16,4,1024]{2,1,0:T(4,128)(2,1)}), bf16[16,4,1024]{2,1,0:T(4,128)(2,1)}, u32[]{:S(2)}, u32[]{:S(2)}) async-start(bf16[16,4,1024]{2,1,0:T(4,128)(2,1)} %reshape.503), calls=%async_computation | async-start | bytes 262144 | tf_op jit(solution)/shard_map/all_to_all | solution.py:75
  86.3 4.3 %collective-permute-start.4 = (bf16[16,4,1024]{2,1,0:T(4,128)(2,1)S(1)}, bf16[16,4,1024]{2,1,0:T(4,128)(2,1)}, u32[]{:S(2)}, u32[]{:S(2)}) collective-permute-start(bf16[16,4,1024]{2,1,0:T(4,128)(2,1)S(1)} %all-to-all-done.4), channel_id=1, source_target_pairs={{0,1},{1,0},{2,3},{3,2},{4,5},{5,4},{6,7},{7,6},{8,9},{9,8},{10,11... | collective-permute-start | bytes 393224 | tf_op jit(solution)/shard_map/ppermute | solution.py:11
  90.6 2.5 collective-permute-start.6
  93.1 1.3 all-to-all-done
  94.4 3.9 %collective-permute-start = (bf16[16,4,1024]{2,1,0:T(4,128)(2,1)}, bf16[16,4,1024]{2,1,0:T(4,128)(2,1)S(1)}, u32[]{:S(2)}, u32[]{:S(2)}) collective-permute-start(bf16[16,4,1024]{2,1,0:T(4,128)(2,1)} %all-to-all-done), channel_id=1, source_target_pairs={{0,1},{1,0},{2,3},{3,2},{4,5},{5,4},{6,7},{7,6},{8,9},{9,8},{10,11... | collective-permute-start | bytes 393224 | tf_op jit(solution)/shard_map/ppermute | solution.py:11
  98.3 0.9 broadcast_select_fusion.5
  99.6 1.4 multiply_convert_fusion.12
  101.0 1.0 broadcast_select_fusion.3
  102.0 3.9 %collective-permute-done = bf16[16,4,1024]{2,1,0:T(4,128)(2,1)S(1)} collective-permute-done((bf16[16,4,1024]{2,1,0:T(4,128)(2,1)}, bf16[16,4,1024]{2,1,0:T(4,128)(2,1)S(1)}, u32[]{:S(2)}, u32[]{:S(2)}) %collective-permute-start) | collective-permute-done | bytes 131104 | tf_op jit(solution)/shard_map/ppermute | solution.py:11
  105.9 0.9 broadcast_select_fusion.7
  108.4 0.9 broadcast_select_fusion.1
  112.7 2.1 pad_maximum_fusion
  114.8 3.5 %copy.78 = f32[1024,768]{1,0:T(8,128)} copy(f32[1024,768]{0,1:T(8,128)} %pad_maximum_fusion) | data formatting | bytes 6291456
  119.4 0.8 convert_reduce_fusion.3
  120.2 0.8 convert_reduce_fusion.1
  122.5 0.8 copy.106
  123.3 1.9 collective-permute-start.1
  126.7 0.8 copy.105
  127.5 4.8 %collective-permute-start.3 = (f32[16,4,1024]{2,1,0:T(4,128)}, f32[16,4,1024]{2,1,0:T(4,128)}, u32[]{:S(2)}, u32[]{:S(2)}) collective-permute-start(f32[16,4,1024]{2,1,0:T(4,128)} %bitcast.223), channel_id=1, source_target_pairs={{0,1},{1,0},{2,3},{3,2},{4,5},{5,4},{6,7},{7,6},{8,9},{9,8},{10,11... | collective-permute-start | bytes 786440 | tf_op jit(solution)/shard_map/ppermute | solution.py:11
  133.8 0.8 copy.103
  134.6 1.9 collective-permute-start.7
  136.5 14.2 %collective-permute-done.1 = f32[16,4,1024]{2,1,0:T(4,128)} collective-permute-done((f32[16,4,1024]{2,1,0:T(4,128)}, f32[16,4,1024]{2,1,0:T(4,128)}, u32[]{:S(2)}, u32[]{:S(2)}) %collective-permute-start.1) | collective-permute-done | bytes 262176 | tf_op jit(solution)/shard_map/ppermute | solution.py:11
  150.8 1.8 bitcast_add_fusion.3
  152.5 8.1 %all-to-all-start.1 = ((f32[16,4,1024]{2,1,0:T(4,128)}), f32[16,4,1024]{2,1,0:T(4,128)S(1)}, u32[]{:S(2)}, u32[]{:S(2)}) async-start(f32[16,4,1024]{2,1,0:T(4,128)} %bitcast_add_fusion.3), calls=%async_computation.1 | async-start | bytes 524288 | tf_op jit(solution)/shard_map/all_to_all | solution.py:105
  160.9 1.8 bitcast_add_fusion.2
  162.7 10.1 %all-to-all-done.1 = f32[16,4,1024]{2,1,0:T(4,128)S(1)} async-done(((f32[16,4,1024]{2,1,0:T(4,128)}), f32[16,4,1024]{2,1,0:T(4,128)S(1)}, u32[]{:S(2)}, u32[]{:S(2)}) %all-to-all-start.1) | async-done | bytes 262176 | tf_op jit(solution)/shard_map/all_to_all | solution.py:105
  172.8 6.7 %all-to-all-start.3 = ((f32[16,4,1024]{2,1,0:T(4,128)}), f32[16,4,1024]{2,1,0:T(4,128)S(1)}, u32[]{:S(2)}, u32[]{:S(2)}) async-start(f32[16,4,1024]{2,1,0:T(4,128)} %bitcast_add_fusion.2), calls=%async_computation.3 | async-start | bytes 524288 | tf_op jit(solution)/shard_map/all_to_all | solution.py:105
  180.8 4.3 %collective-permute-start.5 = (f32[16,4,1024]{2,1,0:T(4,128)S(1)}, f32[16,4,1024]{2,1,0:T(4,128)S(1)}, u32[]{:S(2)}, u32[]{:S(2)}) collective-permute-start(f32[16,4,1024]{2,1,0:T(4,128)S(1)} %bitcast.264), channel_id=1, source_target_pairs={{0,1},{1,0},{2,3},{3,2},{4,5},{5,4},{6,7},{7,6},{8,9},{9,8},{10,11... | collective-permute-start | bytes 786440 | tf_op jit(solution)/shard_map/ppermute | solution.py:11
  185.1 0.8 bitcast_add_fusion
  185.9 5.4 %all-to-all-done.3 = f32[16,4,1024]{2,1,0:T(4,128)S(1)} async-done(((f32[16,4,1024]{2,1,0:T(4,128)}), f32[16,4,1024]{2,1,0:T(4,128)S(1)}, u32[]{:S(2)}, u32[]{:S(2)}) %all-to-all-start.3) | async-done | bytes 262176 | tf_op jit(solution)/shard_map/all_to_all | solution.py:105
  191.3 6.2 %all-to-all-start.7 = ((f32[16,4,1024]{2,1,0:T(4,128)}), f32[16,4,1024]{2,1,0:T(4,128)S(1)}, u32[]{:S(2)}, u32[]{:S(2)}) async-start(f32[16,4,1024]{2,1,0:T(4,128)} %bitcast_add_fusion), calls=%async_computation.7 | async-start | bytes 524288 | tf_op jit(solution)/shard_map/all_to_all | solution.py:105
  197.7 2.1 collective-permute-done.5
  199.8 0.8 bitcast_add_fusion.1
  200.6 9.3 %all-to-all-done.7 = f32[16,4,1024]{2,1,0:T(4,128)S(1)} async-done(((f32[16,4,1024]{2,1,0:T(4,128)}), f32[16,4,1024]{2,1,0:T(4,128)S(1)}, u32[]{:S(2)}, u32[]{:S(2)}) %all-to-all-start.7) | async-done | bytes 262176 | tf_op jit(solution)/shard_map/all_to_all | solution.py:105
  209.9 6.6 %all-to-all-start.5 = ((f32[16,4,1024]{2,1,0:T(4,128)}), f32[16,4,1024]{2,1,0:T(4,128)S(1)}, u32[]{:S(2)}, u32[]{:S(2)}) async-start(f32[16,4,1024]{2,1,0:T(4,128)} %bitcast_add_fusion.1), calls=%async_computation.5 | async-start | bytes 524288 | tf_op jit(solution)/shard_map/all_to_all | solution.py:105
  218.3 9.9 %all-to-all-done.5 = f32[16,4,1024]{2,1,0:T(4,128)S(1)} async-done(((f32[16,4,1024]{2,1,0:T(4,128)}), f32[16,4,1024]{2,1,0:T(4,128)S(1)}, u32[]{:S(2)}, u32[]{:S(2)}) %all-to-all-start.5) | async-done | bytes 262176 | tf_op jit(solution)/shard_map/all_to_all | solution.py:105
  230.0 0.9 pad_maximum_fusion.1
  230.9 15.2 %reduce-scatter.4.cloned.1.call-done = f32[32,768]{1,0:T(8,128)} async-done(((f32[1024,768]{1,0:T(8,128)}), f32[32,768]{1,0:T(8,128)}) %reduce-scatter.4.cloned.1.call-update) | async-done | bytes 98320
  246.1 0.8 fusion.105
  247.8 0.7 copy.76
  (259 shorter events, 28.4 us)
Async XLA Ops:
  7.2 28.8 %copy-start = (bf16[1024,256]{1,0:T(8,128)(2,1)S(1)}, bf16[1024,256]{1,0:T(8,128)(2,1)}, u32[]{:S(2)}) copy-start(bf16[1024,256]{1,0:T(8,128)(2,1)} %param.15) | copy-start | bytes 1572868
  7.2 9.0 %copy-start.11 = (bf16[4,64,1024]{2,1,0:T(8,128)(2,1)S(1)}, bf16[4,64,1024]{2,1,0:T(8,128)(2,1)}, u32[]{:S(2)}) copy-start(bf16[4,64,1024]{2,1,0:T(8,128)(2,1)} %param.11) | copy-start | bytes 1572868
  8.1 0.6 copy-start.7
  8.2 26.9 %copy-start.28 = (s32[512]{0:T(512)}, s32[512]{0:T(512)S(1)}, u32[]{:S(2)}) copy-start(s32[512]{0:T(512)S(1)} %eq.268) | copy-start | bytes 6148
  8.7 6.3 %copy-start.3 = (s32[1,64,8]{2,1,0:T(8,128)}, s32[1,64,8]{2,1,0:T(8,128)S(1)}, u32[]{:S(2)}) copy-start(s32[1,64,8]{2,1,0:T(8,128)S(1)} %copy.89) | copy-start | bytes 6148
  8.8 27.5 %copy-start.24 = (s32[512]{0:T(512)}, s32[512]{0:T(512)S(1)}, u32[]{:S(2)}) copy-start(s32[512]{0:T(512)S(1)} %eq.285) | copy-start | bytes 6148
  8.8 27.2 %copy-start.2 = (bf16[4,128,1024]{2,1,0:T(8,128)(2,1)S(1)}, bf16[4,128,1024]{2,1,0:T(8,128)(2,1)}, u32[]{:S(2)}) copy-start(bf16[4,128,1024]{2,1,0:T(8,128)(2,1)} %param.14) | copy-start | bytes 3145732
  10.3 0.6 copy-start.32
  13.5 2.5 copy-start.18
  13.8 0.6 copy-start.36
  17.7 28.6 %all-to-all-start.2 = ((bf16[16,4,1024]{2,1,0:T(4,128)(2,1)}), bf16[16,4,1024]{2,1,0:T(4,128)(2,1)S(1)}, u32[]{:S(2)}, u32[]{:S(2)}) async-start(bf16[16,4,1024]{2,1,0:T(4,128)(2,1)} %reshape.509), calls=%async_computation.2 | async-start | bytes 262144 | tf_op jit(solution)/shard_map/all_to_all | solution.py:75
  31.1 2.1 copy-start.9
  31.2 1.6 copy-start.30
  32.5 4.1 %copy-start.20 = (s32[8,4,128]{2,0,1:T(8,128)}, s32[8,4,128]{2,0,1:T(8,128)S(1)}, u32[]{:S(2)}) copy-start(s32[8,4,128]{2,0,1:T(8,128)S(1)} %reduce-window.52) | copy-start | bytes 49156
  32.7 0.6 copy-start.38
  33.4 4.3 %copy-start.5 = (s32[1,64,8]{2,1,0:T(8,128)}, s32[1,64,8]{2,1,0:T(8,128)S(1)}, u32[]{:S(2)}) copy-start(s32[1,64,8]{2,1,0:T(8,128)S(1)} %copy.91) | copy-start | bytes 6148
  33.5 6.5 %copy-start.26 = (s32[512]{0:T(512)}, s32[512]{0:T(512)S(1)}, u32[]{:S(2)}) copy-start(s32[512]{0:T(512)S(1)} %eq.317) | copy-start | bytes 6148
  34.7 1.8 copy-start.16
  35.0 0.6 copy-start.34
  40.4 5.7 %copy-start.1 = (bf16[1024,256]{1,0:T(8,128)(2,1)S(1)}, bf16[1024,256]{1,0:T(8,128)(2,1)}, u32[]{:S(2)}) copy-start(bf16[1024,256]{1,0:T(8,128)(2,1)} %param.16) | copy-start | bytes 1572868
  46.3 18.1 %all-to-all-start.6 = ((bf16[16,4,1024]{2,1,0:T(4,128)(2,1)}), bf16[16,4,1024]{2,1,0:T(4,128)(2,1)S(1)}, u32[]{:S(2)}, u32[]{:S(2)}) async-start(bf16[16,4,1024]{2,1,0:T(4,128)(2,1)} %reshape.521), calls=%async_computation.6 | async-start | bytes 262144 | tf_op jit(solution)/shard_map/all_to_all | solution.py:75
  64.4 15.0 %all-to-all-start.4 = ((bf16[16,4,1024]{2,1,0:T(4,128)(2,1)}), bf16[16,4,1024]{2,1,0:T(4,128)(2,1)S(1)}, u32[]{:S(2)}, u32[]{:S(2)}) async-start(bf16[16,4,1024]{2,1,0:T(4,128)(2,1)} %reshape.515), calls=%async_computation.4 | async-start | bytes 262144 | tf_op jit(solution)/shard_map/all_to_all | solution.py:75
  70.6 27.6 %collective-permute-start.2 = (bf16[16,4,1024]{2,1,0:T(4,128)(2,1)S(1)}, bf16[16,4,1024]{2,1,0:T(4,128)(2,1)}, u32[]{:S(2)}, u32[]{:S(2)}) collective-permute-start(bf16[16,4,1024]{2,1,0:T(4,128)(2,1)S(1)} %all-to-all-done.2), channel_id=1, source_target_pairs={{0,1},{1,0},{2,3},{3,2},{4,5},{5,4},{6,7},{7,6},{8,9},{9,8},{10,11... | collective-permute-start | bytes 393224 | tf_op jit(solution)/shard_map/ppermute | solution.py:11
  79.4 15.0 %all-to-all-start = ((bf16[16,4,1024]{2,1,0:T(4,128)(2,1)}), bf16[16,4,1024]{2,1,0:T(4,128)(2,1)}, u32[]{:S(2)}, u32[]{:S(2)}) async-start(bf16[16,4,1024]{2,1,0:T(4,128)(2,1)} %reshape.503), calls=%async_computation | async-start | bytes 262144 | tf_op jit(solution)/shard_map/all_to_all | solution.py:75
  86.0 160.1 %reduce-scatter.4.cloned.1.call-start = ((), (), s32[]{:S(2)}) async-start(), calls=%async_computation.9 | async-start | bytes 3244032
  86.3 14.7 %collective-permute-start.4 = (bf16[16,4,1024]{2,1,0:T(4,128)(2,1)S(1)}, bf16[16,4,1024]{2,1,0:T(4,128)(2,1)}, u32[]{:S(2)}, u32[]{:S(2)}) collective-permute-start(bf16[16,4,1024]{2,1,0:T(4,128)(2,1)S(1)} %all-to-all-done.4), channel_id=1, source_target_pairs={{0,1},{1,0},{2,3},{3,2},{4,5},{5,4},{6,7},{7,6},{8,9},{9,8},{10,11... | collective-permute-start | bytes 393224 | tf_op jit(solution)/shard_map/ppermute | solution.py:11
  90.6 17.8 %collective-permute-start.6 = (bf16[16,4,1024]{2,1,0:T(4,128)(2,1)S(1)}, bf16[16,4,1024]{2,1,0:T(4,128)(2,1)}, u32[]{:S(2)}, u32[]{:S(2)}) collective-permute-start(bf16[16,4,1024]{2,1,0:T(4,128)(2,1)S(1)} %all-to-all-done.6), channel_id=1, source_target_pairs={{0,1},{1,0},{2,3},{3,2},{4,5},{5,4},{6,7},{7,6},{8,9},{9,8},{10,11... | collective-permute-start | bytes 393224 | tf_op jit(solution)/shard_map/ppermute | solution.py:11
  94.4 12.5 %copy-start.40 = (bf16[256,1024]{1,0:T(8,128)(2,1)S(1)}, bf16[256,1024]{1,0:T(8,128)(2,1)}, u32[]{:S(2)}) copy-start(bf16[256,1024]{1,0:T(8,128)(2,1)} %param.17) | copy-start | bytes 1572868
  94.4 11.6 %collective-permute-start = (bf16[16,4,1024]{2,1,0:T(4,128)(2,1)}, bf16[16,4,1024]{2,1,0:T(4,128)(2,1)S(1)}, u32[]{:S(2)}, u32[]{:S(2)}) collective-permute-start(bf16[16,4,1024]{2,1,0:T(4,128)(2,1)} %all-to-all-done), channel_id=1, source_target_pairs={{0,1},{1,0},{2,3},{3,2},{4,5},{5,4},{6,7},{7,6},{8,9},{9,8},{10,11... | collective-permute-start | bytes 393224 | tf_op jit(solution)/shard_map/ppermute | solution.py:11
  101.0 9.7 %copy-start.12 = (bf16[128,256]{1,0:T(8,128)(2,1)}, bf16[128,256]{1,0:T(8,128)(2,1)S(1)}, u32[]{:S(2)}) copy-start(bf16[128,256]{1,0:T(8,128)(2,1)S(1)} %get-tuple-element.58) | copy-start | bytes 196612
  101.0 10.7 %copy-start.14 = (bf16[128,256]{1,0:T(8,128)(2,1)}, bf16[128,256]{1,0:T(8,128)(2,1)S(1)}, u32[]{:S(2)}) copy-start(bf16[128,256]{1,0:T(8,128)(2,1)S(1)} %get-tuple-element.59) | copy-start | bytes 196612
  118.3 0.7 copy-start.19
  118.3 0.7 copy-start.29
  118.3 0.7 copy-start.37
  118.3 0.9 copy-start.21
  118.3 0.9 copy-start.31
  118.3 0.9 copy-start.39
  118.3 1.1 copy-start.8
  118.3 1.9 copy-start.10
  118.4 6.8 %copy-start.15 = (bf16[128,256]{1,0:T(8,128)(2,1)S(1)}, bf16[128,256]{1,0:T(8,128)(2,1)}, u32[]{:S(2)}) copy-start(bf16[128,256]{1,0:T(8,128)(2,1)} %copy-done.14) | copy-start | bytes 196612
  121.0 4.5 %copy-start.13 = (bf16[128,256]{1,0:T(8,128)(2,1)S(1)}, bf16[128,256]{1,0:T(8,128)(2,1)}, u32[]{:S(2)}) copy-start(bf16[128,256]{1,0:T(8,128)(2,1)} %copy-done.12) | copy-start | bytes 196612
  123.3 27.5 %collective-permute-start.1 = (f32[16,4,1024]{2,1,0:T(4,128)}, f32[16,4,1024]{2,1,0:T(4,128)}, u32[]{:S(2)}, u32[]{:S(2)}) collective-permute-start(f32[16,4,1024]{2,1,0:T(4,128)} %bitcast.224), channel_id=1, source_target_pairs={{0,1},{1,0},{2,3},{3,2},{4,5},{5,4},{6,7},{7,6},{8,9},{9,8},{10,11... | collective-permute-start | bytes 786440 | tf_op jit(solution)/shard_map/ppermute | solution.py:11
  127.5 33.4 %collective-permute-start.3 = (f32[16,4,1024]{2,1,0:T(4,128)}, f32[16,4,1024]{2,1,0:T(4,128)}, u32[]{:S(2)}, u32[]{:S(2)}) collective-permute-start(f32[16,4,1024]{2,1,0:T(4,128)} %bitcast.223), channel_id=1, source_target_pairs={{0,1},{1,0},{2,3},{3,2},{4,5},{5,4},{6,7},{7,6},{8,9},{9,8},{10,11... | collective-permute-start | bytes 786440 | tf_op jit(solution)/shard_map/ppermute | solution.py:11
  134.6 50.5 %collective-permute-start.7 = (f32[16,4,1024]{2,1,0:T(4,128)}, f32[16,4,1024]{2,1,0:T(4,128)S(1)}, u32[]{:S(2)}, u32[]{:S(2)}) collective-permute-start(f32[16,4,1024]{2,1,0:T(4,128)} %bitcast.221), channel_id=1, source_target_pairs={{0,1},{1,0},{2,3},{3,2},{4,5},{5,4},{6,7},{7,6},{8,9},{9,8},{10,11... | collective-permute-start | bytes 786440 | tf_op jit(solution)/shard_map/ppermute | solution.py:11
  152.5 20.2 %all-to-all-start.1 = ((f32[16,4,1024]{2,1,0:T(4,128)}), f32[16,4,1024]{2,1,0:T(4,128)S(1)}, u32[]{:S(2)}, u32[]{:S(2)}) async-start(f32[16,4,1024]{2,1,0:T(4,128)} %bitcast_add_fusion.3), calls=%async_computation.1 | async-start | bytes 524288 | tf_op jit(solution)/shard_map/all_to_all | solution.py:105
  162.7 34.8 %copy-start.25 = (s32[512]{0:T(512)S(1)}, s32[512]{0:T(512)}, u32[]{:S(2)}) copy-start(s32[512]{0:T(512)} %copy-done.24) | copy-start | bytes 6148
  162.7 34.8 %copy-start.33 = (s32[8,4]{0,1:T(4,128)S(1)}, s32[8,4]{0,1:T(4,128)}, u32[]{:S(2)}) copy-start(s32[8,4]{0,1:T(4,128)} %copy-done.32) | copy-start | bytes 388
  162.7 35.0 %copy-start.4 = (s32[1,64,8]{2,1,0:T(8,128)S(1)}, s32[1,64,8]{2,1,0:T(8,128)}, u32[]{:S(2)}) copy-start(s32[1,64,8]{2,1,0:T(8,128)} %copy-done.3) | copy-start | bytes 6148
  172.8 18.5 %all-to-all-start.3 = ((f32[16,4,1024]{2,1,0:T(4,128)}), f32[16,4,1024]{2,1,0:T(4,128)S(1)}, u32[]{:S(2)}, u32[]{:S(2)}) async-start(f32[16,4,1024]{2,1,0:T(4,128)} %bitcast_add_fusion.2), calls=%async_computation.3 | async-start | bytes 524288 | tf_op jit(solution)/shard_map/all_to_all | solution.py:105
  179.5 37.1 %copy-start.17 = (s32[8,4,128]{2,0,1:T(8,128)S(1)}, s32[8,4,128]{2,0,1:T(8,128)}, u32[]{:S(2)}) copy-start(s32[8,4,128]{2,0,1:T(8,128)} %copy-done.16) | copy-start | bytes 49156
  179.5 37.1 %copy-start.27 = (s32[512]{0:T(512)S(1)}, s32[512]{0:T(512)}, u32[]{:S(2)}) copy-start(s32[512]{0:T(512)} %copy-done.26) | copy-start | bytes 6148
  179.5 37.1 %copy-start.35 = (s32[8,4]{0,1:T(4,128)S(1)}, s32[8,4]{0,1:T(4,128)}, u32[]{:S(2)}) copy-start(s32[8,4]{0,1:T(4,128)} %copy-done.34) | copy-start | bytes 388
  179.8 37.1 %copy-start.6 = (s32[1,64,8]{2,1,0:T(8,128)S(1)}, s32[1,64,8]{2,1,0:T(8,128)}, u32[]{:S(2)}) copy-start(s32[1,64,8]{2,1,0:T(8,128)} %copy-done.5) | copy-start | bytes 6148
  180.8 19.0 %collective-permute-start.5 = (f32[16,4,1024]{2,1,0:T(4,128)S(1)}, f32[16,4,1024]{2,1,0:T(4,128)S(1)}, u32[]{:S(2)}, u32[]{:S(2)}) collective-permute-start(f32[16,4,1024]{2,1,0:T(4,128)S(1)} %bitcast.264), channel_id=1, source_target_pairs={{0,1},{1,0},{2,3},{3,2},{4,5},{5,4},{6,7},{7,6},{8,9},{9,8},{10,11... | collective-permute-start | bytes 786440 | tf_op jit(solution)/shard_map/ppermute | solution.py:11
  185.9 42.7 %copy-start.23 = (f32[64,64]{1,0:T(8,128)S(1)}, f32[64,64]{1,0:T(8,128)}, u32[]{:S(2)}) copy-start(f32[64,64]{1,0:T(8,128)} %convert_reduce_fusion.3) | copy-start | bytes 49156
  191.3 18.7 %all-to-all-start.7 = ((f32[16,4,1024]{2,1,0:T(4,128)}), f32[16,4,1024]{2,1,0:T(4,128)S(1)}, u32[]{:S(2)}, u32[]{:S(2)}) async-start(f32[16,4,1024]{2,1,0:T(4,128)} %bitcast_add_fusion), calls=%async_computation.7 | async-start | bytes 524288 | tf_op jit(solution)/shard_map/all_to_all | solution.py:105
  200.6 29.1 %copy-start.22 = (f32[64,64]{1,0:T(8,128)S(1)}, f32[64,64]{1,0:T(8,128)}, u32[]{:S(2)}) copy-start(f32[64,64]{1,0:T(8,128)} %convert_reduce_fusion.1) | copy-start | bytes 49156
  209.9 18.2 %all-to-all-start.5 = ((f32[16,4,1024]{2,1,0:T(4,128)}), f32[16,4,1024]{2,1,0:T(4,128)S(1)}, u32[]{:S(2)}, u32[]{:S(2)}) async-start(f32[16,4,1024]{2,1,0:T(4,128)} %bitcast_add_fusion.1), calls=%async_computation.5 | async-start | bytes 524288 | tf_op jit(solution)/shard_map/all_to_all | solution.py:105
Sparse Core Ops, SparseCore 0:
  118.5 127.5 reduce-scatter.3
where the time goes:
time: 257 us; the launch traced here: 256 us
  starting transfers between devices  91.1 us (35%)
  waiting for transfers between devices  84.1 us (33%)
  local copies, waits for them, and re-layouts  32.4 us (13%)
  other arithmetic  21.1 us (8%)
  between operations  15.3 us (6%)
  matrix products  12.2 us (5%)
    all_to_all x4, starting transfers between devices, per_device(): lax.all_to_all(sending.reshape(groups, half_caps, model_width), 'expert',...  35.6 us
    all_to_all x4, waiting for transfers between devices, per_device(): lax.all_to_all(kept_part + partner, 'expert', split_axis=0, concat_axis=0...  34.7 us
    ppermute x8, starting transfers between devices, swapped(): lax.ppermute(x, axis, [(i, i ^ 1 << stride) for i in range(lax.axis_size(...  27.8 us
    all_to_all x4, starting transfers between devices, per_device(): lax.all_to_all(kept_part + partner, 'expert', split_axis=0, concat_axis=0...  27.6 us
    ppermute x8, waiting for transfers between devices, swapped(): lax.ppermute(x, axis, [(i, i ^ 1 << stride) for i in range(lax.axis_size(...  20.3 us
    unnamed x2, waiting for transfers between devices  15.2 us
    all_to_all x4, waiting for transfers between devices, per_device(): lax.all_to_all(sending.reshape(groups, half_caps, model_width), 'expert',...  13.9 us
    unnamed x97, local copies, waits for them, and re-layouts  11.4 us
  transfers between devices with their start and end apart: 17, of which 11 were waited for; matrix products, arithmetic and copies ran while one was open for 16% of the time, Pallas kernels for 0%

commit v1 on v0

v1 whole, which is shorter than its diff:
```python
import jax
import jax.numpy as jnp
from jax import lax
from jax.experimental import pallas as pl
from jax.experimental.pallas import tpu as pltpu
from jax.sharding import Mesh
from jax.sharding import PartitionSpec as P

TOPK = 8
CAPS = 8
DP = ("zl", "y", "core")
DP_CHIPS = ("zl", "y")
EXPERT = ("x", "zq", "zp")
ALL_DP = DP + EXPERT
VMEM = pl.BlockSpec(memory_space=pltpu.VMEM)


def dot(left, right, contract):
    return lax.dot_general(
        left, right, ((contract[:1], contract[1:]), ((), ())), preferred_element_type=jnp.float32
    )


def call(body, outs, flops, name, specs):
    return pl.pallas_call(
        body,
        out_shape=outs,
        in_specs=specs,
        out_specs=jax.tree.map(lambda _: VMEM, outs),
        name=name,
        compiler_params=pltpu.CompilerParams(vmem_limit_bytes=20 * 1024 * 1024),
        cost_estimate=pl.CostEstimate(flops=flops, bytes_accessed=4 << 20, transcendentals=0),
    )


def route_body(ids_ref, probs_ref, grad_ref, send_ref, pick_ref):
    micro, _, tokens = ids_ref.shape
    holders = send_ref.shape[0]
    rows = holders * CAPS
    row = lax.broadcasted_iota(jnp.int32, (rows, tokens), 0)
    expert = row // (2 * CAPS)
    slot = (row % CAPS).astype(jnp.float32)
    earlier = (
        lax.broadcasted_iota(jnp.int32, (tokens, tokens), 0)
        < lax.broadcasted_iota(jnp.int32, (tokens, tokens), 1)
    ).astype(jnp.bfloat16)
    for m in range(micro):
        weight = jnp.zeros((rows, tokens), jnp.float32)
        live = jnp.zeros((rows, tokens), jnp.float32)
        for k in range(TOPK):
            named = ids_ref[m, k : k + 1, :] == expert
            weight = jnp.where(named, probs_ref[m, k : k + 1, :].astype(jnp.float32), weight)
            live = jnp.where(named, 1.0, live)
        rank = dot(live.astype(jnp.bfloat16), earlier, (1, 0))
        chosen = jnp.logical_and(live > 0.0, rank == slot)
        pick_ref[m] = chosen.astype(jnp.bfloat16)
        scaled = dot(jnp.where(chosen, weight, 0.0).astype(jnp.bfloat16), grad_ref[m], (1, 0))
        send_ref[:, m * CAPS : (m + 1) * CAPS, :] = scaled.astype(jnp.bfloat16).reshape(
            holders, CAPS, -1
        )


def forward_body(x_ref, gate_w_ref, up_w_ref, hidden_ref, to_up_ref, to_gate_ref):
    for m in range(x_ref.shape[0]):
        x = x_ref[m]
        gate = dot(x, gate_w_ref[...], (1, 0))
        up = dot(x, up_w_ref[...], (1, 0))
        sigmoid = jax.nn.sigmoid(gate)
        activated = gate * sigmoid
        hidden_ref[m] = (activated * up).astype(jnp.bfloat16)
        to_up_ref[m] = activated
        to_gate_ref[m] = up * sigmoid * (1.0 + gate * (1.0 - sigmoid))


def slot_body(
    got_ref, to_up_ref, to_gate_ref, gate_w_ref, up_w_ref, down_w_ref, back_ref, d_gate_ref, d_up_ref
):
    holders = got_ref.shape[0]
    for m in range(to_up_ref.shape[0]):
        part = slice(m * CAPS, (m + 1) * CAPS)
        scaled = got_ref[:, part, :].reshape(holders * CAPS, -1)
        d_hidden = dot(scaled, down_w_ref[...], (1, 1))
        d_gate = (d_hidden * to_gate_ref[m]).astype(jnp.bfloat16)
        d_up = (d_hidden * to_up_ref[m]).astype(jnp.bfloat16)
        d_gate_ref[m] = d_gate
        d_up_ref[m] = d_up
        back = dot(d_gate, gate_w_ref[...], (1, 1)) + dot(d_up, up_w_ref[...], (1, 1))
        back_ref[:, part, :] = back.astype(jnp.bfloat16).reshape(holders, CAPS, -1)


def weight_body(core_ref, x_ref, got_ref, hidden_ref, d_gate_ref, d_up_ref, keep_ref, give_ref, all_ref):
    micro, slots, width = x_ref.shape
    chips, rows, _ = keep_ref.shape
    cols = hidden_ref.shape[2]
    core = core_ref[0]
    x = x_ref[...].reshape(micro * slots, width)
    got = jnp.concatenate(
        [
            got_ref[:, m * CAPS : (m + 1) * CAPS, :].reshape(slots, width)
            for m in range(micro)
        ],
        axis=0,
    )
    terms = ((x, d_gate_ref), (x, d_up_ref), (got, hidden_ref))
    for k, (left, right_ref) in enumerate(terms):
        total = dot(left, right_ref[...].reshape(micro * slots, cols), (0, 0))
        all_ref[:, :, :, k * cols : (k + 1) * cols] = total.reshape(chips, 2, rows, cols)
    keep_ref[...] = all_ref[:, pl.ds(core, 1)].reshape(keep_ref.shape)
    give_ref[...] = all_ref[:, pl.ds(1 - core, 1)].reshape(give_ref.shape)


def mix_body(pick_ref, back_ref, out_ref):
    holders = back_ref.shape[0]
    for m in range(pick_ref.shape[0]):
        rows = back_ref[:, m * CAPS : (m + 1) * CAPS, :].reshape(holders * CAPS, -1)
        out_ref[m] = dot(pick_ref[m], rows, (0, 0)).astype(jnp.bfloat16)


def total_body(factor, terms_ref, gate_ref, up_ref, down_ref):
    total = terms_ref[0].astype(jnp.float32)
    for k in range(1, terms_ref.shape[0]):
        total = total + terms_ref[k].astype(jnp.float32)
    total = total * factor
    cols = gate_ref.shape[1]
    gate_ref[...] = total[:, :cols]
    up_ref[...] = total[:, cols : 2 * cols]
    down_ref[...] = total[:, 2 * cols :]


def per_device(grad_out, routes, route_probs, dispatched, w_gate, w_up, w_down):
    micro, tokens, width = grad_out.shape
    slots = dispatched.shape[1]
    cols = w_gate.shape[1]
    holders = lax.axis_size("x") * lax.axis_size("zq") * lax.axis_size("zp")
    chips = lax.axis_size("zl") * lax.axis_size("y")
    rows = width // (2 * chips)
    bf16, f32 = jnp.bfloat16, jnp.float32
    shape = jax.ShapeDtypeStruct

    send, pick = call(
        route_body,
        (
            shape((holders, micro * CAPS, width), bf16),
            shape((micro, holders * CAPS, tokens), bf16),
        ),
        1 << 27,
        "route",
        [VMEM] * 3,
    )(jnp.swapaxes(routes, 1, 2), jnp.swapaxes(route_probs, 1, 2), grad_out)
    with jax.named_scope("dispatch"):
        got = lax.all_to_all(send, EXPERT, 0, 0, tiled=True)
    hidden, to_up, to_gate = call(
        forward_body,
        (
            shape((micro, slots, cols), bf16),
            shape((micro, slots, cols), f32),
            shape((micro, slots, cols), f32),
        ),
        1 << 30,
        "forward",
        [VMEM] * 3,
    )(dispatched, w_gate, w_up)
    back_send, d_gate, d_up = call(
        slot_body,
        (
            shape((holders, micro * CAPS, width), bf16),
            shape((micro, slots, cols), bf16),
            shape((micro, slots, cols), bf16),
        ),
        1 << 30,
        "slots",
        [VMEM] * 6,
    )(got, to_up, to_gate, w_gate, w_up, w_down)
    with jax.named_scope("back"):
        back = lax.all_to_all(back_send, EXPERT, 0, 0, tiled=True)
    core = lax.axis_index("core").astype(jnp.int32).reshape(1)
    keep, give = pl.pallas_call(
        weight_body,
        out_shape=(shape((chips, rows, 3 * cols), f32), shape((chips, rows, 3 * cols), f32)),
        in_specs=[pl.BlockSpec(memory_space=pltpu.SMEM)] + [VMEM] * 5,
        out_specs=(VMEM, VMEM),
        scratch_shapes=[pltpu.VMEM((chips, 2, rows, 3 * cols), f32)],
        name="weights",
        compiler_params=pltpu.CompilerParams(vmem_limit_bytes=20 * 1024 * 1024),
        cost_estimate=pl.CostEstimate(flops=1 << 30, bytes_accessed=8 << 20, transcendentals=0),
    )(core, dispatched, got, hidden, d_gate, d_up)
    with jax.named_scope("cores"):
        other = lax.ppermute(give, "core", [(0, 1), (1, 0)])
    chip_sum = (keep + other).astype(bf16)
    with jax.named_scope("reduce"):
        terms = lax.all_to_all(chip_sum, DP_CHIPS, 0, 0, tiled=True)
    grad_in = call(
        mix_body, shape((micro, tokens, width), bf16), 1 << 27, "mix", [VMEM] * 2
    )(pick, back)
    factor = 1.0 / (micro * chips * 2)
    grads = call(
        lambda *refs: total_body(factor, *refs),
        tuple(shape((rows, cols), f32) for _ in range(3)),
        1 << 20,
        "total",
        [VMEM],
    )(terms)
    return (grad_in, *grads)


def solution(mesh):
    fine = Mesh(mesh.devices.reshape(2, 8, 2, 4, 2, 2), DP + EXPERT)
    tokens = P(None, ALL_DP, None)
    return jax.shard_map(
        per_device,
        mesh=fine,
        in_specs=(tokens, tokens, tokens, tokens, P(None, EXPERT), P(None, EXPERT), P(EXPERT, None)),
        out_specs=(tokens, P(DP, EXPERT), P(DP, EXPERT), P(DP, EXPERT)),
        check_vma=False,
    )
```

time: 257 us -> 117 us (0.46)
  the two profiles are of different devices: /device:TPU:4 before, /device:TPU:8 now
where the time goes in v1:
time: 117 us; the launch traced here: 116 us
  waiting for transfers between devices  59.3 us (51%)
  starting transfers between devices  35.2 us (30%)
  local copies, waits for them, and re-layouts  10.5 us (9%)
  Pallas kernels  9.25 us (8%)
    all_to_all x1, waiting for transfers between devices, per_device(): got = lax.all_to_all(send, EXPERT, 0, 0, tiled=True)  21.1 us
    all_to_all x1, waiting for transfers between devices, per_device(): terms = lax.all_to_all(chip_sum, DP_CHIPS, 0, 0, tiled=True)  19.7 us
    all_to_all x1, waiting for transfers between devices, per_device(): back = lax.all_to_all(back_send, EXPERT, 0, 0, tiled=True)  15.1 us
    all_to_all x1, starting transfers between devices, per_device(): terms = lax.all_to_all(chip_sum, DP_CHIPS, 0, 0, tiled=True)  13.2 us
    all_to_all x1, starting transfers between devices, per_device(): got = lax.all_to_all(send, EXPERT, 0, 0, tiled=True)  12.9 us
    unnamed x30, local copies, waits for them, and re-layouts  10.5 us
    all_to_all x1, starting transfers between devices, per_device(): back = lax.all_to_all(back_send, EXPERT, 0, 0, tiled=True)  7.19 us
    pallas_call x1, Pallas kernels, per_device(): call(slot_body, (shape((holders, micro * CAPS, width), bf16), shape((micr...  3.39 us
  transfers between devices with their start and end apart: 4, of which 4 were waited for; matrix products, arithmetic and copies ran while one was open for 1% of the time, Pallas kernels for 3%

profile of v1, /device:TPU:8, one launch (start us, length us, event | category | flops | bytes accessed | tf_op | source)
XLA Modules:
  0.0 116.1 jit_solution(14675186683196710001)
XLA Ops:
  0.6 0.0 copy-start
  0.6 1.0 copy-done
  1.7 0.0 copy-start.1
  1.7 0.7 copy-done.1
  2.4 0.0 copy-start.2
  2.4 0.7 copy-done.2
  3.1 0.0 copy-start.3
  3.1 0.0 copy-start.4
  3.1 0.0 copy-start.5
  3.1 2.0 %route.1 = (bf16[16,32,1024]{2,1,0:T(8,128)(2,1)}, bf16[4,128,64]{2,1,0:T(8,128)(2,1)S(1)}) custom-call(s32[4,8,64]{2,1,0:T(8,128)S(1)} %bitcast.3, bf16[4,8,64]{2,1,0:T(8,128)(2,1)S(1)} %bitcast.4, bf16[4,64,1024]{2,1,0:T(8,128)(2,1)S(1)} %copy-done), custom_call_target="tpu_custom_call" | custom-call | flops 134217728 | bytes 4194304 | tf_op jit(solution)/shard_map/route/pallas_call | solution.py:140
  5.1 12.9 %all-to-all-start = ((bf16[16,32,1024]{2,1,0:T(8,128)(2,1)}), bf16[16,32,1024]{2,1,0:T(8,128)(2,1)S(1)}, u32[]{:S(2)}, u32[]{:S(2)}) async-start(bf16[16,32,1024]{2,1,0:T(8,128)(2,1)} %get-tuple-element.18), calls=%async_computation | async-start | bytes 2097152 | tf_op jit(solution)/shard_map/dispatch/all_to_all | solution.py:151
  18.0 0.0 copy-done.3
  18.0 0.0 copy-done.4
  18.0 0.0 copy-done.5
  18.0 0.7 forward.1
  18.8 0.0 copy-start.7
  18.8 0.8 copy-done.7
  19.6 0.0 copy-start.9
  19.6 0.8 copy-done.9
  20.4 0.0 copy-start.13
  20.4 0.7 copy-done.13
  21.1 21.1 %all-to-all-done.got_ref = bf16[16,32,1024]{2,1,0:T(8,128)(2,1)S(1)} async-done(((bf16[16,32,1024]{2,1,0:T(8,128)(2,1)}), bf16[16,32,1024]{2,1,0:T(8,128)(2,1)S(1)}, u32[]{:S(2)}, u32[]{:S(2)}) %all-to-all-start) | async-done | bytes 1048608 | tf_op jit(solution)/shard_map/dispatch/all_to_all | solution.py:151
  42.2 0.0 copy-start.6
  42.2 1.0 copy-done.6
  43.3 0.0 copy-start.8
  43.3 1.0 copy-done.8
  44.3 0.0 copy-start.10
  44.3 1.0 copy-done.10
  45.3 3.4 %slots.1 = (bf16[16,32,1024]{2,1,0:T(8,128)(2,1)}, bf16[4,128,256]{2,1,0:T(8,128)(2,1)S(1)}, bf16[4,128,256]{2,1,0:T(8,128)(2,1)S(1)}) custom-call(bf16[16,32,1024]{2,1,0:T(8,128)(2,1)S(1)} %all-to-all-done.got_ref, f32[4,128,256]{2,1,0:T(8,128)S(1)} %copy-done.8, f32[4,128,256]{2,1,0:T(8,128)S(1)} %copy-done.10, bf16[1024,256]{1,0:T(8,128)(2,1)S(1)} %copy-done.4, ...), custom_call_target="tpu_custom_call" | custom-call | flops 1073741824 | bytes 4194304 | tf_op jit(solution)/shard_map/slots/pallas_call | solution.py:163
  48.7 0.0 copy-start.11
  48.7 0.7 copy-done.11
  49.4 7.2 %all-to-all-start.1 = ((bf16[16,32,1024]{2,1,0:T(8,128)(2,1)}), bf16[16,32,1024]{2,1,0:T(8,128)(2,1)S(1)}, u32[]{:S(2)}, u32[]{:S(2)}) async-start(bf16[16,32,1024]{2,1,0:T(8,128)(2,1)} %get-tuple-element.21), calls=%async_computation.1 | async-start | bytes 2097152 | tf_op jit(solution)/shard_map/back/all_to_all | solution.py:175
  56.6 0.0 copy-start.12
  56.6 0.9 copy-done.12
  57.6 0.0 copy-start.14
  57.6 0.9 copy-done.14
  58.5 1.3 %weights.1 = (f32[16,32,768]{2,1,0:T(8,128)S(1)}, f32[16,32,768]{2,1,0:T(8,128)S(1)}) custom-call(s32[1]{0:T(128)} %bitcast.2.core_ref, bf16[4,128,1024]{2,1,0:T(8,128)(2,1)S(1)} %copy-done.3, bf16[16,32,1024]{2,1,0:T(8,128)(2,1)S(1)} %all-to-all-done.got_ref, bf16[4,128,256]{2,1,0:T(8,128)(2,1)S(1)} %copy-done.14, ...), custom_call_target="tpu_custom_call" | custom-call | flops 1073741824 | bytes 8388608 | tf_op jit(solution)/shard_map/weights/pallas_call | solution.py:177
  59.8 1.9 %collective-permute-start = (f32[16,32,768]{2,1,0:T(8,128)S(1)}, f32[16,32,768]{2,1,0:T(8,128)S(1)}, u32[]{:S(2)}, u32[]{:S(2)}) collective-permute-start(f32[16,32,768]{2,1,0:T(8,128)S(1)} %get-tuple-element.26), channel_id=1, source_target_pairs={{0,16},{16,0},{1,17},{17,1},{2,18},{18,2},{3,19},{19,3},{4,20},{20... | collective-permute-start | bytes 4718600 | tf_op jit(solution)/shard_map/cores/ppermute | solution.py:188
  61.7 3.4 %collective-permute-done = f32[16,32,768]{2,1,0:T(8,128)S(1)} collective-permute-done((f32[16,32,768]{2,1,0:T(8,128)S(1)}, f32[16,32,768]{2,1,0:T(8,128)S(1)}, u32[]{:S(2)}, u32[]{:S(2)}) %collective-permute-start) | collective-permute-done | bytes 1572896 | tf_op jit(solution)/shard_map/cores/ppermute | solution.py:188
  65.1 1.1 add_convert_fusion
  66.2 15.1 %all-to-all-done.1.back_ref = bf16[16,32,1024]{2,1,0:T(8,128)(2,1)S(1)} async-done(((bf16[16,32,1024]{2,1,0:T(8,128)(2,1)}), bf16[16,32,1024]{2,1,0:T(8,128)(2,1)S(1)}, u32[]{:S(2)}, u32[]{:S(2)}) %all-to-all-start.1) | async-done | bytes 1048608 | tf_op jit(solution)/shard_map/back/all_to_all | solution.py:175
  81.3 13.2 %all-to-all-start.2 = ((bf16[16,32,768]{2,1,0:T(8,128)(2,1)}), bf16[16,32,768]{2,1,0:T(8,128)(2,1)S(1)}, u32[]{:S(2)}, u32[]{:S(2)}) async-start(bf16[16,32,768]{2,1,0:T(8,128)(2,1)} %add_convert_fusion), calls=%async_computation.2 | async-start | bytes 1572864 | tf_op jit(solution)/shard_map/reduce/all_to_all | solution.py:191
  94.5 1.1 mix.1
  95.6 19.7 %all-to-all-done.2.refs_0_ = bf16[16,32,768]{2,1,0:T(8,128)(2,1)S(1)} async-done(((bf16[16,32,768]{2,1,0:T(8,128)(2,1)}), bf16[16,32,768]{2,1,0:T(8,128)(2,1)S(1)}, u32[]{:S(2)}, u32[]{:S(2)}) %all-to-all-start.2) | async-done | bytes 786464 | tf_op jit(solution)/shard_map/reduce/all_to_all | solution.py:191
  115.3 0.7 total.1
Async XLA Ops:
  0.6 1.0 copy-start
  1.7 0.7 copy-start.1
  2.4 0.7 copy-start.2
  3.1 14.9 %copy-start.3 = (bf16[4,128,1024]{2,1,0:T(8,128)(2,1)S(1)}, bf16[4,128,1024]{2,1,0:T(8,128)(2,1)}, u32[]{:S(2)}) copy-start(bf16[4,128,1024]{2,1,0:T(8,128)(2,1)} %x_ref.3) | copy-start | bytes 3145732
  3.1 14.9 %copy-start.4 = (bf16[1024,256]{1,0:T(8,128)(2,1)S(1)}, bf16[1024,256]{1,0:T(8,128)(2,1)}, u32[]{:S(2)}) copy-start(bf16[1024,256]{1,0:T(8,128)(2,1)} %gate_w_ref.3) | copy-start | bytes 1572868
  3.1 14.9 %copy-start.5 = (bf16[1024,256]{1,0:T(8,128)(2,1)S(1)}, bf16[1024,256]{1,0:T(8,128)(2,1)}, u32[]{:S(2)}) copy-start(bf16[1024,256]{1,0:T(8,128)(2,1)} %up_w_ref.3) | copy-start | bytes 1572868
  5.1 37.1 %all-to-all-start = ((bf16[16,32,1024]{2,1,0:T(8,128)(2,1)}), bf16[16,32,1024]{2,1,0:T(8,128)(2,1)S(1)}, u32[]{:S(2)}, u32[]{:S(2)}) async-start(bf16[16,32,1024]{2,1,0:T(8,128)(2,1)} %get-tuple-element.18), calls=%async_computation | async-start | bytes 2097152 | tf_op jit(solution)/shard_map/dispatch/all_to_all | solution.py:151
  18.8 0.8 copy-start.7
  19.6 0.8 copy-start.9
  20.4 0.7 copy-start.13
  42.2 1.0 copy-start.6
  43.3 1.0 copy-start.8
  44.3 1.0 copy-start.10
  48.7 0.7 copy-start.11
  49.4 31.8 %all-to-all-start.1 = ((bf16[16,32,1024]{2,1,0:T(8,128)(2,1)}), bf16[16,32,1024]{2,1,0:T(8,128)(2,1)S(1)}, u32[]{:S(2)}, u32[]{:S(2)}) async-start(bf16[16,32,1024]{2,1,0:T(8,128)(2,1)} %get-tuple-element.21), calls=%async_computation.1 | async-start | bytes 2097152 | tf_op jit(solution)/shard_map/back/all_to_all | solution.py:175
  56.6 1.0 copy-start.12
  57.6 0.9 copy-start.14
  59.8 5.3 %collective-permute-start = (f32[16,32,768]{2,1,0:T(8,128)S(1)}, f32[16,32,768]{2,1,0:T(8,128)S(1)}, u32[]{:S(2)}, u32[]{:S(2)}) collective-permute-start(f32[16,32,768]{2,1,0:T(8,128)S(1)} %get-tuple-element.26), channel_id=1, source_target_pairs={{0,16},{16,0},{1,17},{17,1},{2,18},{18,2},{3,19},{19,3},{4,20},{20... | collective-permute-start | bytes 4718600 | tf_op jit(solution)/shard_map/cores/ppermute | solution.py:188
  81.3 34.0 %all-to-all-start.2 = ((bf16[16,32,768]{2,1,0:T(8,128)(2,1)}), bf16[16,32,768]{2,1,0:T(8,128)(2,1)S(1)}, u32[]{:S(2)}, u32[]{:S(2)}) async-start(bf16[16,32,768]{2,1,0:T(8,128)(2,1)} %add_convert_fusion), calls=%async_computation.2 | async-start | bytes 1572864 | tf_op jit(solution)/shard_map/reduce/all_to_all | solution.py:191

commit v2 on v1

v2 whole, which is shorter than its diff:
```python
import jax
import jax.numpy as jnp
from jax import lax
from jax.experimental import pallas as pl
from jax.experimental.pallas import tpu as pltpu
from jax.sharding import Mesh
from jax.sharding import PartitionSpec as P

TOPK = 8
CAPS = 8
DP = ("zl", "y", "core")
EXPERT = ("x", "zq", "zp")
STAGES = (("core", 1), ("y", 1), ("y", 2))
LAST = (4, 8, 12)
ALL_DP = DP + EXPERT
VMEM = pl.BlockSpec(memory_space=pltpu.VMEM)
HBM = pl.BlockSpec(memory_space=pltpu.HBM)


def dot(left, right, contract):
    return lax.dot_general(
        left, right, ((contract[:1], contract[1:]), ((), ())), preferred_element_type=jnp.float32
    )


def call(body, outs, flops, specs, scratch=(), to_hbm=0, limit=20):
    return pl.pallas_call(
        body,
        out_shape=outs,
        in_specs=specs,
        out_specs=tuple(HBM if k < to_hbm else VMEM for k in range(len(outs))),
        scratch_shapes=list(scratch),
        compiler_params=pltpu.CompilerParams(vmem_limit_bytes=limit * 1024 * 1024),
        cost_estimate=pl.CostEstimate(flops=flops, bytes_accessed=4 << 20, transcendentals=0),
    )


def route_body(
    ids_hbm,
    probs_hbm,
    grad_hbm,
    send_hbm,
    pick_ref,
    ids_ref,
    probs_ref,
    grad_ref,
    send_ref,
    sems,
    out_sems,
):
    copies = [
        pltpu.make_async_copy(source, goal, sems.at[k])
        for k, (source, goal) in enumerate(
            ((ids_hbm, ids_ref), (probs_hbm, probs_ref), (grad_hbm, grad_ref))
        )
    ]
    for copy in copies:
        copy.start()
    micro, _, tokens = ids_ref.shape
    holders = send_ref.shape[1]
    rows = holders * CAPS
    row = lax.broadcasted_iota(jnp.int32, (rows, tokens), 0)
    expert = row // (2 * CAPS)
    slot = (row % CAPS).astype(jnp.float32)
    earlier = (
        lax.broadcasted_iota(jnp.int32, (tokens, tokens), 0)
        < lax.broadcasted_iota(jnp.int32, (tokens, tokens), 1)
    ).astype(jnp.bfloat16)
    for copy in copies[:2]:
        copy.wait()
    weights = []
    for m in range(micro):
        weight = jnp.zeros((rows, tokens), jnp.float32)
        live = jnp.zeros((rows, tokens), jnp.float32)
        for k in range(TOPK):
            named = ids_ref[m, k : k + 1, :] == expert
            weight = jnp.where(named, probs_ref[m, k : k + 1, :].astype(jnp.float32), weight)
            live = jnp.where(named, 1.0, live)
        rank = dot(live.astype(jnp.bfloat16), earlier, (1, 0))
        chosen = jnp.logical_and(live > 0.0, rank == slot)
        pick_ref[m] = chosen.astype(jnp.bfloat16)
        weights.append(jnp.where(chosen, weight, 0.0).astype(jnp.bfloat16))
    copies[2].wait()
    puts = []
    for m in range(micro):
        scaled = dot(weights[m], grad_ref[m], (1, 0))
        send_ref[m] = scaled.astype(jnp.bfloat16).reshape(holders, CAPS, -1)
        put = pltpu.make_async_copy(
            send_ref.at[m], send_hbm.at[:, pl.ds(m * CAPS, CAPS), :], out_sems.at[m]
        )
        put.start()
        puts.append(put)
    for put in puts:
        put.wait()


def weight_body(
    got_ref,
    x_ref,
    gate_w_ref,
    up_w_ref,
    down_w_ref,
    d_gate_ref,
    d_up_ref,
    keep_ref,
    give_ref,
    got_all_ref,
    all_ref,
):
    micro, slots, width = x_ref.shape
    pieces, rows, _ = all_ref.shape
    cols = gate_w_ref.shape[1]
    x = x_ref[...].reshape(micro * slots, width)
    for m in range(micro):
        got_all_ref[m * slots : (m + 1) * slots] = got_ref[
            :, m * CAPS : (m + 1) * CAPS, :
        ].reshape(slots, width)
    gate = dot(x, gate_w_ref[...], (1, 0))
    up = dot(x, up_w_ref[...], (1, 0))
    sigmoid = jax.nn.sigmoid(gate)
    activated = gate * sigmoid
    hidden = (activated * up).astype(jnp.bfloat16)
    to_gate = up * sigmoid * (1.0 + gate * (1.0 - sigmoid))
    d_hidden = dot(got_all_ref[...], down_w_ref[...], (1, 1))
    d_gate_ref[...] = (d_hidden * to_gate).astype(jnp.bfloat16)
    d_up_ref[...] = (d_hidden * activated).astype(jnp.bfloat16)
    terms = ((x, d_gate_ref[...]), (x, d_up_ref[...]), (got_all_ref[...], hidden))
    for k, (left, right) in enumerate(terms):
        total = dot(left, right, (0, 0))
        all_ref[:, :, k * cols : (k + 1) * cols] = total.reshape(pieces, rows, cols)
    me = lax.axis_index(DP)
    for k in range(pieces // 2):
        keep_ref[k] = all_ref[me ^ (2 * k)]
        give_ref[k] = all_ref[me ^ (2 * k + 1)].astype(jnp.bfloat16)


def slot_body(d_gate_ref, d_up_ref, gate_w_ref, up_w_ref, back_hbm, back_ref, sems):
    micro, holders, _, width = back_ref.shape
    slots = holders * CAPS
    puts = []
    for m in range(micro):
        rows = slice(m * slots, (m + 1) * slots)
        back = dot(d_gate_ref[rows], gate_w_ref[...], (1, 1)) + dot(
            d_up_ref[rows], up_w_ref[...], (1, 1)
        )
        back_ref[m] = back.astype(jnp.bfloat16).reshape(holders, CAPS, width)
        put = pltpu.make_async_copy(
            back_ref.at[m], back_hbm.at[:, pl.ds(m * CAPS, CAPS), :], sems.at[m]
        )
        put.start()
        puts.append(put)
    for put in puts:
        put.wait()


def halve_body(keep_ref, other_ref, next_keep_ref, next_give_ref):
    for k in range(next_keep_ref.shape[0]):
        next_keep_ref[k] = keep_ref[2 * k] + other_ref[2 * k].astype(jnp.float32)
        next_give_ref[k] = (
            keep_ref[2 * k + 1] + other_ref[2 * k + 1].astype(jnp.float32)
        ).astype(jnp.bfloat16)


def spread_body(keep_ref, other_ref, next_keep_ref, *give_refs):
    next_keep_ref[...] = keep_ref[0] + other_ref[0].astype(jnp.float32)
    for k, give_ref in enumerate(give_refs, 1):
        give_ref[...] = (keep_ref[k] + other_ref[k].astype(jnp.float32)).astype(jnp.bfloat16)


def mix_body(pick_ref, back_ref, out_ref):
    holders = back_ref.shape[0]
    for m in range(pick_ref.shape[0]):
        rows = back_ref[:, m * CAPS : (m + 1) * CAPS, :].reshape(holders * CAPS, -1)
        out_ref[m] = dot(pick_ref[m], rows, (0, 0)).astype(jnp.bfloat16)


def total_body(factor, keep_ref, *refs):
    other_refs, out_refs = refs[:-3], refs[-3:]
    cols = out_refs[0].shape[1]
    total = keep_ref[...]
    for other_ref in other_refs:
        total = total + other_ref[...].astype(jnp.float32)
    total = total * factor
    for k, out_ref in enumerate(out_refs):
        out_ref[...] = total[:, k * cols : (k + 1) * cols]


def flipped(size, flip):
    return [(i, i ^ flip) for i in range(size)]


def per_device(grad_out, routes, route_probs, dispatched, w_gate, w_up, w_down):
    micro, tokens, width = grad_out.shape
    slots = dispatched.shape[1]
    cols = w_gate.shape[1]
    holders = lax.axis_size(EXPERT)
    pieces = lax.axis_size(DP)
    rows = width // pieces
    bf16, f32 = jnp.bfloat16, jnp.float32
    shape = jax.ShapeDtypeStruct

    send, pick = call(
        route_body,
        (
            shape((holders, micro * CAPS, width), bf16),
            shape((micro, holders * CAPS, tokens), bf16),
        ),
        1 << 27,
        [HBM] * 3,
        [
            pltpu.VMEM((micro, TOPK, tokens), jnp.int32),
            pltpu.VMEM((micro, TOPK, tokens), bf16),
            pltpu.VMEM(grad_out.shape, bf16),
            pltpu.VMEM((micro, holders, CAPS, width), bf16),
            pltpu.SemaphoreType.DMA((3,)),
            pltpu.SemaphoreType.DMA((micro,)),
        ],
        1,
        60,
    )(jnp.swapaxes(routes, 1, 2), jnp.swapaxes(route_probs, 1, 2), grad_out)
    got = lax.all_to_all(send, EXPERT, 0, 0, tiled=True)
    def lot(count):
        return count, rows, 3 * cols

    d_gate, d_up, keep, give = call(
        weight_body,
        (
            shape((micro * slots, cols), bf16),
            shape((micro * slots, cols), bf16),
            shape(lot(pieces // 2), f32),
            shape(lot(pieces // 2), bf16),
        ),
        1 << 31,
        [VMEM] * 5,
        [pltpu.VMEM((micro * slots, width), bf16), pltpu.VMEM(lot(pieces), f32)],
    )(got, dispatched, w_gate, w_up, w_down)
    (back_send,) = call(
        slot_body,
        (shape((holders, micro * CAPS, width), bf16),),
        1 << 30,
        [VMEM] * 4,
        [
            pltpu.VMEM((micro, holders, CAPS, width), bf16),
            pltpu.SemaphoreType.DMA((micro,)),
        ],
        1,
    )(d_gate, d_up, w_gate, w_up)
    back = lax.all_to_all(back_send, EXPERT, 0, 0, tiled=True)
    for axis, flip in STAGES:
        other = lax.ppermute(give, axis, flipped(lax.axis_size(axis), flip))
        if (axis, flip) == STAGES[-1]:
            break
        half = lot(keep.shape[0] // 2)
        keep, give = call(
            halve_body, (shape(half, f32), shape(half, bf16)), 1 << 20, [VMEM] * 2
        )(keep, other)
    keep, *gives = call(
        spread_body,
        (shape(lot(1)[1:], f32), *[shape(lot(1)[1:], bf16)] * len(LAST)),
        1 << 20,
        [VMEM] * 2,
    )(keep, other)
    others = []
    for give, flip in zip(gives, LAST):
        others.append(lax.ppermute(give, ("zl", "y"), flipped(lax.axis_size(("zl", "y")), flip)))
    (grad_in,) = call(
        mix_body, (shape((micro, tokens, width), bf16),), 1 << 27, [VMEM] * 2
    )(pick, back)
    factor = 1.0 / (micro * pieces)
    grads = call(
        lambda *refs: total_body(factor, *refs),
        tuple(shape((rows, cols), f32) for _ in range(3)),
        1 << 20,
        [VMEM] * (1 + len(others)),
    )(keep, *others)
    return (grad_in, *grads)


def solution(mesh):
    fine = Mesh(mesh.devices.reshape(2, 8, 2, 4, 2, 2), DP + EXPERT)
    tokens = P(None, ALL_DP, None)
    return jax.shard_map(
        per_device,
        mesh=fine,
        in_specs=(tokens, tokens, tokens, tokens, P(None, EXPERT), P(None, EXPERT), P(EXPERT, None)),
        out_specs=(tokens, P(DP, EXPERT), P(DP, EXPERT), P(DP, EXPERT)),
        check_vma=False,
    )
```

time: 117 us -> 112 us (0.957)
  the two profiles are of different devices: /device:TPU:8 before, /device:TPU:2 now
where the time goes in v2:
time: 112 us; the launch traced here: 111 us
  blocking collectives  41.6 us (37%)
  waiting for transfers between devices  29.2 us (26%)
  starting transfers between devices  28.6 us (26%)
  Pallas kernels  9.88 us (9%)
    all_to_all x1, blocking collectives, per_device(): got = lax.all_to_all(send, EXPERT, 0, 0, tiled=True)  41.6 us
    ppermute x3, waiting for transfers between devices, per_device(): other = lax.ppermute(give, axis, flipped(lax.axis_size(axis), flip))  20.4 us
    ppermute x3, starting transfers between devices, per_device(): lax.ppermute(give, ('zl', 'y'), flipped(lax.axis_size(('zl', 'y')), flip))  15 us
    ppermute x3, starting transfers between devices, per_device(): other = lax.ppermute(give, axis, flipped(lax.axis_size(axis), flip))  10 us
    ppermute x3, waiting for transfers between devices, per_device(): lax.ppermute(give, ('zl', 'y'), flipped(lax.axis_size(('zl', 'y')), flip))  8.85 us
    all_to_all x1, starting transfers between devices, per_device(): back = lax.all_to_all(back_send, EXPERT, 0, 0, tiled=True)  3.55 us
    pallas_call x1, Pallas kernels, per_device(): call(route_body, (shape((holders, micro * CAPS, width), bf16), shape((mic...  3.17 us
    pallas_call x1, Pallas kernels, per_device(): call(weight_body, (shape((micro * slots, cols), bf16), shape((micro * slo...  2.68 us
  transfers between devices with their start and end apart: 7, of which 5 were waited for; matrix products, arithmetic and copies ran while one was open for 0% of the time, Pallas kernels for 1%

profile of v2, /device:TPU:2, one launch (start us, length us, event | category | flops | bytes accessed | tf_op | source)
XLA Modules:
  0.0 111.1 jit_solution(15250853993163994016)
XLA Ops:
  0.6 0.0 copy-start.3
  0.6 3.2 %shard_map.102 = (bf16[16,32,1024]{2,1,0:T(8,128)(2,1)}, bf16[4,128,64]{2,1,0:T(8,128)(2,1)}) custom-call(s32[4,8,64]{2,1,0:T(8,128)} %bitcast.2, bf16[4,8,64]{2,1,0:T(8,128)(2,1)} %bitcast.3, bf16[4,64,1024]{2,1,0:T(8,128)(2,1)} %grad_hbm.1), custom_call_target="tpu_custom_call" | custom-call | flops 134217728 | bytes 4194304 | tf_op jit(solution)/shard_map/pallas_call | solution.py:202
  3.8 0.0 copy-start.2
  3.8 0.0 copy-start.4
  3.8 0.0 copy-start.5
  3.9 41.6 %all_to_all.10.got_ref = bf16[16,32,1024]{2,1,0:T(8,128)(2,1)S(1)} all-to-all(bf16[16,32,1024]{2,1,0:T(8,128)(2,1)} %get-tuple-element.22), channel_id=1, replica_groups=mesh['zl'=2,'y'=8,'core'=2,'x'=4,'zq'=2,'zp'=2] {'x','zq','zp'}, dimensions={0} | all-to-all | bytes 2097152 | tf_op jit(solution)/shard_map/all_to_all | solution.py:221
  45.5 0.0 copy-done.3
  45.5 0.0 copy-done.2
  45.5 0.0 copy-done.4
  45.5 0.0 copy-done.5
  45.5 2.7 %shard_map.103 = (bf16[512,256]{1,0:T(8,128)(2,1)S(1)}, bf16[512,256]{1,0:T(8,128)(2,1)S(1)}, f32[16,32,768]{2,1,0:T(8,128)S(1)}, bf16[16,32,768]{2,1,0:T(8,128)(2,1)S(1)}) custom-call(bf16[16,32,1024]{2,1,0:T(8,128)(2,1)S(1)} %all_to_all.10.got_ref, bf16[4,128,1024]{2,1,0:T(8,128)(2,1)S(1)} %copy-done.2, bf16[1024,256]{1,0:T(8,128)(2,1)S(1)} %copy-done.4, ...), custom_call_target="tpu_custom_call" | custom-call | flops 2147483648 | bytes 4194304 | tf_op jit(solution)/shard_map/pallas_call | solution.py:225
  48.2 2.0 %shard_map.104 = bf16[16,32,1024]{2,1,0:T(8,128)(2,1)S(1)} custom-call(bf16[512,256]{1,0:T(8,128)(2,1)S(1)} %get-tuple-element.23.d_gate_ref, bf16[512,256]{1,0:T(8,128)(2,1)S(1)} %get-tuple-element.24.d_up_ref, bf16[1024,256]{1,0:T(8,128)(2,1)S(1)} %copy-done.4, bf16[1024,256]{1,0:T(8,128)(2,1)S(1)} %copy-done.5), custom_call_target="tpu_custom_call" | custom-call | flops 1073741824 | bytes 4194304 | tf_op jit(solution)/shard_map/pallas_call | solution.py:237
  50.2 0.0 copy-start
  50.2 1.0 copy-done
  51.2 3.5 %all-to-all-start.1 = ((bf16[16,32,1024]{2,1,0:T(8,128)(2,1)}), bf16[16,32,1024]{2,1,0:T(8,128)(2,1)S(1)}, u32[]{:S(2)}, u32[]{:S(2)}) async-start(bf16[16,32,1024]{2,1,0:T(8,128)(2,1)} %copy-done), calls=%async_computation.1 | async-start | bytes 2097152 | tf_op jit(solution)/shard_map/all_to_all | solution.py:248
  54.8 1.9 %collective-permute-start = (bf16[16,32,768]{2,1,0:T(8,128)(2,1)S(1)}, bf16[16,32,768]{2,1,0:T(8,128)(2,1)S(1)}, u32[]{:S(2)}, u32[]{:S(2)}) collective-permute-start(bf16[16,32,768]{2,1,0:T(8,128)(2,1)S(1)} %get-tuple-element.26), channel_id=1, source_target_pairs={{0,16},{16,0},{1,17},{17,1},{2,18},{18,2},{3,19},{19,3},{4,20},{20... | collective-permute-start | bytes 2359304 | tf_op jit(solution)/shard_map/ppermute | solution.py:250
  56.7 2.3 %collective-permute-done.other_ref = bf16[16,32,768]{2,1,0:T(8,128)(2,1)S(1)} collective-permute-done((bf16[16,32,768]{2,1,0:T(8,128)(2,1)S(1)}, bf16[16,32,768]{2,1,0:T(8,128)(2,1)S(1)}, u32[]{:S(2)}, u32[]{:S(2)}) %collective-permute-start) | collective-permute-done | bytes 786464 | tf_op jit(solution)/shard_map/ppermute | solution.py:250
  58.9 0.1 shard_map.106
  59.1 0.0 copy-start.1
  59.1 3.6 %collective-permute-start.1 = (bf16[8,32,768]{2,1,0:T(8,128)(2,1)S(1)}, bf16[8,32,768]{2,1,0:T(8,128)(2,1)S(1)}, u32[]{:S(2)}, u32[]{:S(2)}) collective-permute-start(bf16[8,32,768]{2,1,0:T(8,128)(2,1)S(1)} %get-tuple-element.28), channel_id=1, source_target_pairs={{0,32},{32,0},{64,96},{96,64},{128,160},{160,128},{192,224},{224,1... | collective-permute-start | bytes 1179656 | tf_op jit(solution)/shard_map/ppermute | solution.py:250
  62.7 9.6 %collective-permute-done.1.other_ref = bf16[8,32,768]{2,1,0:T(8,128)(2,1)S(1)} collective-permute-done((bf16[8,32,768]{2,1,0:T(8,128)(2,1)S(1)}, bf16[8,32,768]{2,1,0:T(8,128)(2,1)S(1)}, u32[]{:S(2)}, u32[]{:S(2)}) %collective-permute-start.1) | collective-permute-done | bytes 393248 | tf_op jit(solution)/shard_map/ppermute | solution.py:250
  72.3 0.1 shard_map.107
  72.3 4.5 %collective-permute-start.2 = (bf16[4,32,768]{2,1,0:T(8,128)(2,1)S(1)}, bf16[4,32,768]{2,1,0:T(8,128)(2,1)S(1)}, u32[]{:S(2)}, u32[]{:S(2)}) collective-permute-start(bf16[4,32,768]{2,1,0:T(8,128)(2,1)S(1)} %get-tuple-element.30), channel_id=1, source_target_pairs={{0,64},{32,96},{64,0},{96,32},{128,192},{160,224},{192,128},{224,1... | collective-permute-start | bytes 589832 | tf_op jit(solution)/shard_map/ppermute | solution.py:250
  76.8 8.6 %collective-permute-done.2.other_ref = bf16[4,32,768]{2,1,0:T(8,128)(2,1)S(1)} collective-permute-done((bf16[4,32,768]{2,1,0:T(8,128)(2,1)S(1)}, bf16[4,32,768]{2,1,0:T(8,128)(2,1)S(1)}, u32[]{:S(2)}, u32[]{:S(2)}) %collective-permute-start.2) | collective-permute-done | bytes 196640 | tf_op jit(solution)/shard_map/ppermute | solution.py:250
  85.5 7.7 %collective-permute-start.3 = (bf16[32,768]{1,0:T(8,128)(2,1)S(1)}, bf16[32,768]{1,0:T(8,128)(2,1)S(1)}, u32[]{:S(2)}, u32[]{:S(2)}) collective-permute-start(bf16[32,768]{1,0:T(8,128)(2,1)S(1)} %get-tuple-element.32), channel_id=1, source_target_pairs={{0,128},{32,160},{64,192},{96,224},{128,0},{160,32},{192,64},{224,... | collective-permute-start | bytes 147464 | tf_op jit(solution)/shard_map/ppermute | solution.py:265
  93.2 5.4 %collective-permute-start.4 = (bf16[32,768]{1,0:T(8,128)(2,1)S(1)}, bf16[32,768]{1,0:T(8,128)(2,1)S(1)}, u32[]{:S(2)}, u32[]{:S(2)}) collective-permute-start(bf16[32,768]{1,0:T(8,128)(2,1)S(1)} %get-tuple-element.33), channel_id=1, source_target_pairs={{0,256},{32,288},{64,320},{96,352},{128,384},{160,416},{192,448},{... | collective-permute-start | bytes 147464 | tf_op jit(solution)/shard_map/ppermute | solution.py:265
  98.6 1.9 %collective-permute-start.5 = (bf16[32,768]{1,0:T(8,128)(2,1)S(1)}, bf16[32,768]{1,0:T(8,128)(2,1)S(1)}, u32[]{:S(2)}, u32[]{:S(2)}) collective-permute-start(bf16[32,768]{1,0:T(8,128)(2,1)S(1)} %get-tuple-element.34), channel_id=1, source_target_pairs={{0,384},{32,416},{64,448},{96,480},{128,256},{160,288},{192,320},{... | collective-permute-start | bytes 147464 | tf_op jit(solution)/shard_map/ppermute | solution.py:265
  100.5 0.0 collective-permute-done.3.refs_1_
  100.5 0.1 collective-permute-done.4.refs_2_
  100.6 8.7 %collective-permute-done.5.refs_3_ = bf16[32,768]{1,0:T(8,128)(2,1)S(1)} collective-permute-done((bf16[32,768]{1,0:T(8,128)(2,1)S(1)}, bf16[32,768]{1,0:T(8,128)(2,1)S(1)}, u32[]{:S(2)}, u32[]{:S(2)}) %collective-permute-start.5) | collective-permute-done | bytes 49184 | tf_op jit(solution)/shard_map/ppermute | solution.py:265
  109.4 0.6 shard_map.109
  110.0 0.0 all-to-all-done.1.back_ref
  110.0 0.0 copy-done.1
  110.0 1.1 %shard_map.105 = bf16[4,64,1024]{2,1,0:T(8,128)(2,1)} custom-call(bf16[4,128,64]{2,1,0:T(8,128)(2,1)S(1)} %copy-done.1, bf16[16,32,1024]{2,1,0:T(8,128)(2,1)S(1)} %all-to-all-done.1.back_ref), custom_call_target="tpu_custom_call" | custom-call | flops 134217728 | bytes 4194304 | tf_op jit(solution)/shard_map/pallas_call | solution.py:266
  (1 shorter events, 0.0 us)
Async XLA Ops:
  0.6 44.8 %copy-start.3 = (bf16[256,1024]{1,0:T(8,128)(2,1)S(1)}, bf16[256,1024]{1,0:T(8,128)(2,1)}, u32[]{:S(2)}) copy-start(bf16[256,1024]{1,0:T(8,128)(2,1)} %down_w_ref.1) | copy-start | bytes 1572868
  3.8 41.7 %copy-start.2 = (bf16[4,128,1024]{2,1,0:T(8,128)(2,1)S(1)}, bf16[4,128,1024]{2,1,0:T(8,128)(2,1)}, u32[]{:S(2)}) copy-start(bf16[4,128,1024]{2,1,0:T(8,128)(2,1)} %x_ref.1) | copy-start | bytes 3145732
  3.8 41.7 %copy-start.4 = (bf16[1024,256]{1,0:T(8,128)(2,1)S(1)}, bf16[1024,256]{1,0:T(8,128)(2,1)}, u32[]{:S(2)}) copy-start(bf16[1024,256]{1,0:T(8,128)(2,1)} %gate_w_ref.3) | copy-start | bytes 1572868
  3.8 41.6 %copy-start.5 = (bf16[1024,256]{1,0:T(8,128)(2,1)S(1)}, bf16[1024,256]{1,0:T(8,128)(2,1)}, u32[]{:S(2)}) copy-start(bf16[1024,256]{1,0:T(8,128)(2,1)} %up_w_ref.3) | copy-start | bytes 1572868
  50.2 1.0 copy-start
  51.2 58.8 %all-to-all-start.1 = ((bf16[16,32,1024]{2,1,0:T(8,128)(2,1)}), bf16[16,32,1024]{2,1,0:T(8,128)(2,1)S(1)}, u32[]{:S(2)}, u32[]{:S(2)}) async-start(bf16[16,32,1024]{2,1,0:T(8,128)(2,1)} %copy-done), calls=%async_computation.1 | async-start | bytes 2097152 | tf_op jit(solution)/shard_map/all_to_all | solution.py:248
  54.8 4.2 %collective-permute-start = (bf16[16,32,768]{2,1,0:T(8,128)(2,1)S(1)}, bf16[16,32,768]{2,1,0:T(8,128)(2,1)S(1)}, u32[]{:S(2)}, u32[]{:S(2)}) collective-permute-start(bf16[16,32,768]{2,1,0:T(8,128)(2,1)S(1)} %get-tuple-element.26), channel_id=1, source_target_pairs={{0,16},{16,0},{1,17},{17,1},{2,18},{18,2},{3,19},{19,3},{4,20},{20... | collective-permute-start | bytes 2359304 | tf_op jit(solution)/shard_map/ppermute | solution.py:250
  59.1 50.9 %copy-start.1 = (bf16[4,128,64]{2,1,0:T(8,128)(2,1)S(1)}, bf16[4,128,64]{2,1,0:T(8,128)(2,1)}, u32[]{:S(2)}) copy-start(bf16[4,128,64]{2,1,0:T(8,128)(2,1)} %get-tuple-element.21.pick_ref) | copy-start | bytes 196612
  59.1 13.2 %collective-permute-start.1 = (bf16[8,32,768]{2,1,0:T(8,128)(2,1)S(1)}, bf16[8,32,768]{2,1,0:T(8,128)(2,1)S(1)}, u32[]{:S(2)}, u32[]{:S(2)}) collective-permute-start(bf16[8,32,768]{2,1,0:T(8,128)(2,1)S(1)} %get-tuple-element.28), channel_id=1, source_target_pairs={{0,32},{32,0},{64,96},{96,64},{128,160},{160,128},{192,224},{224,1... | collective-permute-start | bytes 1179656 | tf_op jit(solution)/shard_map/ppermute | solution.py:250
  72.3 13.1 %collective-permute-start.2 = (bf16[4,32,768]{2,1,0:T(8,128)(2,1)S(1)}, bf16[4,32,768]{2,1,0:T(8,128)(2,1)S(1)}, u32[]{:S(2)}, u32[]{:S(2)}) collective-permute-start(bf16[4,32,768]{2,1,0:T(8,128)(2,1)S(1)} %get-tuple-element.30), channel_id=1, source_target_pairs={{0,64},{32,96},{64,0},{96,32},{128,192},{160,224},{192,128},{224,1... | collective-permute-start | bytes 589832 | tf_op jit(solution)/shard_map/ppermute | solution.py:250
  85.5 15.0 %collective-permute-start.3 = (bf16[32,768]{1,0:T(8,128)(2,1)S(1)}, bf16[32,768]{1,0:T(8,128)(2,1)S(1)}, u32[]{:S(2)}, u32[]{:S(2)}) collective-permute-start(bf16[32,768]{1,0:T(8,128)(2,1)S(1)} %get-tuple-element.32), channel_id=1, source_target_pairs={{0,128},{32,160},{64,192},{96,224},{128,0},{160,32},{192,64},{224,... | collective-permute-start | bytes 147464 | tf_op jit(solution)/shard_map/ppermute | solution.py:265
  93.2 7.4 %collective-permute-start.4 = (bf16[32,768]{1,0:T(8,128)(2,1)S(1)}, bf16[32,768]{1,0:T(8,128)(2,1)S(1)}, u32[]{:S(2)}, u32[]{:S(2)}) collective-permute-start(bf16[32,768]{1,0:T(8,128)(2,1)S(1)} %get-tuple-element.33), channel_id=1, source_target_pairs={{0,256},{32,288},{64,320},{96,352},{128,384},{160,416},{192,448},{... | collective-permute-start | bytes 147464 | tf_op jit(solution)/shard_map/ppermute | solution.py:265
  98.6 10.8 %collective-permute-start.5 = (bf16[32,768]{1,0:T(8,128)(2,1)S(1)}, bf16[32,768]{1,0:T(8,128)(2,1)S(1)}, u32[]{:S(2)}, u32[]{:S(2)}) collective-permute-start(bf16[32,768]{1,0:T(8,128)(2,1)S(1)} %get-tuple-element.34), channel_id=1, source_target_pairs={{0,384},{32,416},{64,448},{96,480},{128,256},{160,288},{192,320},{... | collective-permute-start | bytes 147464 | tf_op jit(solution)/shard_map/ppermute | solution.py:265

commit v3 on v2

--- a/solution.py
+++ b/solution.py
@@ -10,9 +10,22 @@
 CAPS = 8
 DP = ("zl", "y", "core")
 EXPERT = ("x", "zq", "zp")
-STAGES = (("core", 1), ("y", 1), ("y", 2))
-LAST = (4, 8, 12)
 ALL_DP = DP + EXPERT
+
+
+def near(index):
+    return index ^ 1
+
+
+def after(index):
+    return (((index + 1) ^ 1) - 1) & 7
+
+
+def far(index):
+    return index ^ 3 ^ (((index ^ (index >> 1)) & 1) << 2)
+
+
+STAGES = (("core", near), ("y", near), ("y", after), ("y", far), ("zl", near))
 VMEM = pl.BlockSpec(memory_space=pltpu.VMEM)
 HBM = pl.BlockSpec(memory_space=pltpu.HBM)
 
@@ -128,10 +141,14 @@
     for k, (left, right) in enumerate(terms):
         total = dot(left, right, (0, 0))
         all_ref[:, :, k * cols : (k + 1) * cols] = total.reshape(pieces, rows, cols)
-    me = lax.axis_index(DP)
     for k in range(pieces // 2):
-        keep_ref[k] = all_ref[me ^ (2 * k)]
-        give_ref[k] = all_ref[me ^ (2 * k + 1)].astype(jnp.bfloat16)
+        place = {axis: lax.axis_index(axis) for axis in DP}
+        for bit, (axis, partner) in enumerate(STAGES[1:]):
+            if k >> bit & 1:
+                place[axis] = partner(place[axis])
+        chip = (place["zl"] * lax.axis_size("y") + place["y"]) * 2
+        keep_ref[k] = all_ref[chip + place["core"]]
+        give_ref[k] = all_ref[chip + near(place["core"])].astype(jnp.bfloat16)
 
 
 def slot_body(d_gate_ref, d_up_ref, gate_w_ref, up_w_ref, back_hbm, back_ref, sems):
@@ -161,12 +178,6 @@
         ).astype(jnp.bfloat16)
 
 
-def spread_body(keep_ref, other_ref, next_keep_ref, *give_refs):
-    next_keep_ref[...] = keep_ref[0] + other_ref[0].astype(jnp.float32)
-    for k, give_ref in enumerate(give_refs, 1):
-        give_ref[...] = (keep_ref[k] + other_ref[k].astype(jnp.float32)).astype(jnp.bfloat16)
-
-
 def mix_body(pick_ref, back_ref, out_ref):
     holders = back_ref.shape[0]
     for m in range(pick_ref.shape[0]):
@@ -174,19 +185,11 @@
         out_ref[m] = dot(pick_ref[m], rows, (0, 0)).astype(jnp.bfloat16)
 
 
-def total_body(factor, keep_ref, *refs):
-    other_refs, out_refs = refs[:-3], refs[-3:]
+def total_body(factor, keep_ref, other_ref, *out_refs):
     cols = out_refs[0].shape[1]
-    total = keep_ref[...]
-    for other_ref in other_refs:
-        total = total + other_ref[...].astype(jnp.float32)
-    total = total * factor
+    total = (keep_ref[0] + other_ref[0].astype(jnp.float32)) * factor
     for k, out_ref in enumerate(out_refs):
         out_ref[...] = total[:, k * cols : (k + 1) * cols]
-
-
-def flipped(size, flip):
-    return [(i, i ^ flip) for i in range(size)]
 
 
 def per_device(grad_out, routes, route_probs, dispatched, w_gate, w_up, w_down):
@@ -246,23 +249,15 @@
         1,
     )(d_gate, d_up, w_gate, w_up)
     back = lax.all_to_all(back_send, EXPERT, 0, 0, tiled=True)
-    for axis, flip in STAGES:
-        other = lax.ppermute(give, axis, flipped(lax.axis_size(axis), flip))
-        if (axis, flip) == STAGES[-1]:
+    for stage, (axis, partner) in enumerate(STAGES):
+        goals = [(i, partner(i)) for i in range(lax.axis_size(axis))]
+        other = lax.ppermute(give, axis, goals)
+        if stage == len(STAGES) - 1:
             break
         half = lot(keep.shape[0] // 2)
         keep, give = call(
             halve_body, (shape(half, f32), shape(half, bf16)), 1 << 20, [VMEM] * 2
         )(keep, other)
-    keep, *gives = call(
-        spread_body,
-        (shape(lot(1)[1:], f32), *[shape(lot(1)[1:], bf16)] * len(LAST)),
-        1 << 20,
-        [VMEM] * 2,
-    )(keep, other)
-    others = []
-    for give, flip in zip(gives, LAST):
-        others.append(lax.ppermute(give, ("zl", "y"), flipped(lax.axis_size(("zl", "y")), flip)))
     (grad_in,) = call(
         mix_body, (shape((micro, tokens, width), bf16),), 1 << 27, [VMEM] * 2
     )(pick, back)
@@ -271,8 +266,8 @@
         lambda *refs: total_body(factor, *refs),
         tuple(shape((rows, cols), f32) for _ in range(3)),
         1 << 20,
-        [VMEM] * (1 + len(others)),
-    )(keep, *others)
+        [VMEM] * 2,
+    )(keep, other)
     return (grad_in, *grads)
 
 

time: 112 us -> 101 us (0.902)
  the two profiles are of different devices: /device:TPU:2 before, /device:TPU:42 now
where the time goes in v3:
time: 101 us; the launch traced here: 100 us
  blocking collectives  41.6 us (41%)
  waiting for transfers between devices  27 us (27%)
  starting transfers between devices  19.8 us (20%)
  Pallas kernels  9.9 us (10%)
    all_to_all x1, blocking collectives, per_device(): got = lax.all_to_all(send, EXPERT, 0, 0, tiled=True)  41.6 us
    ppermute x5, waiting for transfers between devices, per_device(): other = lax.ppermute(give, axis, goals)  27 us
    ppermute x5, starting transfers between devices, per_device(): other = lax.ppermute(give, axis, goals)  16.3 us
    all_to_all x1, starting transfers between devices, per_device(): back = lax.all_to_all(back_send, EXPERT, 0, 0, tiled=True)  3.55 us
    pallas_call x1, Pallas kernels, per_device(): call(route_body, (shape((holders, micro * CAPS, width), bf16), shape((mic...  3.17 us
    pallas_call x1, Pallas kernels, per_device(): call(weight_body, (shape((micro * slots, cols), bf16), shape((micro * slo...  2.68 us
    pallas_call x1, Pallas kernels, per_device(): call(slot_body, (shape((holders, micro * CAPS, width), bf16),), 1 << 30,...  2.03 us
  transfers between devices with their start and end apart: 6, of which 5 were waited for; matrix products, arithmetic and copies ran while one was open for 0% of the time, Pallas kernels for 1%

profile of v3, /device:TPU:42, one launch (start us, length us, event | category | flops | bytes accessed | tf_op | source)
XLA Modules:
  0.0 100.1 jit_solution(12236402129227145688)
XLA Ops:
  0.6 0.0 copy-start.3
  0.6 3.2 %shard_map.102 = (bf16[16,32,1024]{2,1,0:T(8,128)(2,1)}, bf16[4,128,64]{2,1,0:T(8,128)(2,1)}) custom-call(s32[4,8,64]{2,1,0:T(8,128)} %bitcast.2, bf16[4,8,64]{2,1,0:T(8,128)(2,1)} %bitcast.3, bf16[4,64,1024]{2,1,0:T(8,128)(2,1)} %grad_hbm.1), custom_call_target="tpu_custom_call" | custom-call | flops 134217728 | bytes 4194304 | tf_op jit(solution)/shard_map/pallas_call | solution.py:205
  3.8 0.0 copy-start.2
  3.8 0.0 copy-start.4
  3.8 0.0 copy-start.5
  3.9 41.6 %all_to_all.10.got_ref = bf16[16,32,1024]{2,1,0:T(8,128)(2,1)S(1)} all-to-all(bf16[16,32,1024]{2,1,0:T(8,128)(2,1)} %get-tuple-element.22), channel_id=1, replica_groups=mesh['zl'=2,'y'=8,'core'=2,'x'=4,'zq'=2,'zp'=2] {'x','zq','zp'}, dimensions={0} | all-to-all | bytes 2097152 | tf_op jit(solution)/shard_map/all_to_all | solution.py:224
  45.5 0.0 copy-done.3
  45.5 0.0 copy-done.2
  45.5 0.0 copy-done.4
  45.5 0.0 copy-done.5
  45.5 2.7 %shard_map.103 = (bf16[512,256]{1,0:T(8,128)(2,1)S(1)}, bf16[512,256]{1,0:T(8,128)(2,1)S(1)}, f32[16,32,768]{2,1,0:T(8,128)S(1)}, bf16[16,32,768]{2,1,0:T(8,128)(2,1)S(1)}) custom-call(bf16[16,32,1024]{2,1,0:T(8,128)(2,1)S(1)} %all_to_all.10.got_ref, bf16[4,128,1024]{2,1,0:T(8,128)(2,1)S(1)} %copy-done.2, bf16[1024,256]{1,0:T(8,128)(2,1)S(1)} %copy-done.4, ...), custom_call_target="tpu_custom_call" | custom-call | flops 2147483648 | bytes 4194304 | tf_op jit(solution)/shard_map/pallas_call | solution.py:228
  48.2 2.0 %shard_map.104 = bf16[16,32,1024]{2,1,0:T(8,128)(2,1)S(1)} custom-call(bf16[512,256]{1,0:T(8,128)(2,1)S(1)} %get-tuple-element.23.d_gate_ref, bf16[512,256]{1,0:T(8,128)(2,1)S(1)} %get-tuple-element.24.d_up_ref, bf16[1024,256]{1,0:T(8,128)(2,1)S(1)} %copy-done.4, bf16[1024,256]{1,0:T(8,128)(2,1)S(1)} %copy-done.5), custom_call_target="tpu_custom_call" | custom-call | flops 1073741824 | bytes 4194304 | tf_op jit(solution)/shard_map/pallas_call | solution.py:240
  50.2 0.0 copy-start
  50.2 1.0 copy-done
  51.2 3.5 %all-to-all-start.1 = ((bf16[16,32,1024]{2,1,0:T(8,128)(2,1)}), bf16[16,32,1024]{2,1,0:T(8,128)(2,1)S(1)}, u32[]{:S(2)}, u32[]{:S(2)}) async-start(bf16[16,32,1024]{2,1,0:T(8,128)(2,1)} %copy-done), calls=%async_computation.1 | async-start | bytes 2097152 | tf_op jit(solution)/shard_map/all_to_all | solution.py:251
  54.8 1.9 %collective-permute-start = (bf16[16,32,768]{2,1,0:T(8,128)(2,1)S(1)}, bf16[16,32,768]{2,1,0:T(8,128)(2,1)S(1)}, u32[]{:S(2)}, u32[]{:S(2)}) collective-permute-start(bf16[16,32,768]{2,1,0:T(8,128)(2,1)S(1)} %get-tuple-element.26), channel_id=1, source_target_pairs={{0,16},{16,0},{1,17},{17,1},{2,18},{18,2},{3,19},{19,3},{4,20},{20... | collective-permute-start | bytes 2359304 | tf_op jit(solution)/shard_map/ppermute | solution.py:254
  56.7 2.3 %collective-permute-done.other_ref = bf16[16,32,768]{2,1,0:T(8,128)(2,1)S(1)} collective-permute-done((bf16[16,32,768]{2,1,0:T(8,128)(2,1)S(1)}, bf16[16,32,768]{2,1,0:T(8,128)(2,1)S(1)}, u32[]{:S(2)}, u32[]{:S(2)}) %collective-permute-start) | collective-permute-done | bytes 786464 | tf_op jit(solution)/shard_map/ppermute | solution.py:254
  58.9 0.1 shard_map.106
  59.1 0.0 copy-start.1
  59.1 3.4 %collective-permute-start.1 = (bf16[8,32,768]{2,1,0:T(8,128)(2,1)S(1)}, bf16[8,32,768]{2,1,0:T(8,128)(2,1)S(1)}, u32[]{:S(2)}, u32[]{:S(2)}) collective-permute-start(bf16[8,32,768]{2,1,0:T(8,128)(2,1)S(1)} %get-tuple-element.28), channel_id=1, source_target_pairs={{0,32},{32,0},{64,96},{96,64},{128,160},{160,128},{192,224},{224,1... | collective-permute-start | bytes 1179656 | tf_op jit(solution)/shard_map/ppermute | solution.py:254
  62.5 9.8 %collective-permute-done.1.other_ref = bf16[8,32,768]{2,1,0:T(8,128)(2,1)S(1)} collective-permute-done((bf16[8,32,768]{2,1,0:T(8,128)(2,1)S(1)}, bf16[8,32,768]{2,1,0:T(8,128)(2,1)S(1)}, u32[]{:S(2)}, u32[]{:S(2)}) %collective-permute-start.1) | collective-permute-done | bytes 393248 | tf_op jit(solution)/shard_map/ppermute | solution.py:254
  72.3 0.1 shard_map.107
  72.3 2.6 %collective-permute-start.2 = (bf16[4,32,768]{2,1,0:T(8,128)(2,1)S(1)}, bf16[4,32,768]{2,1,0:T(8,128)(2,1)S(1)}, u32[]{:S(2)}, u32[]{:S(2)}) collective-permute-start(bf16[4,32,768]{2,1,0:T(8,128)(2,1)S(1)} %get-tuple-element.30), channel_id=1, source_target_pairs={{0,224},{32,64},{64,32},{96,128},{128,96},{160,192},{192,160},{224... | collective-permute-start | bytes 589832 | tf_op jit(solution)/shard_map/ppermute | solution.py:254
  74.9 5.4 %collective-permute-done.2.other_ref = bf16[4,32,768]{2,1,0:T(8,128)(2,1)S(1)} collective-permute-done((bf16[4,32,768]{2,1,0:T(8,128)(2,1)S(1)}, bf16[4,32,768]{2,1,0:T(8,128)(2,1)S(1)}, u32[]{:S(2)}, u32[]{:S(2)}) %collective-permute-start.2) | collective-permute-done | bytes 196640 | tf_op jit(solution)/shard_map/ppermute | solution.py:254
  80.3 3.0 %collective-permute-start.3 = (bf16[2,32,768]{2,1,0:T(8,128)(2,1)S(1)}, bf16[2,32,768]{2,1,0:T(8,128)(2,1)S(1)}, u32[]{:S(2)}, u32[]{:S(2)}) collective-permute-start(bf16[2,32,768]{2,1,0:T(8,128)(2,1)S(1)} %get-tuple-element.32), channel_id=1, source_target_pairs={{0,96},{32,192},{64,160},{96,0},{128,224},{160,64},{192,32},{224,1... | collective-permute-start | bytes 294920 | tf_op jit(solution)/shard_map/ppermute | solution.py:254
  83.4 7.5 %collective-permute-done.3.other_ref = bf16[2,32,768]{2,1,0:T(8,128)(2,1)S(1)} collective-permute-done((bf16[2,32,768]{2,1,0:T(8,128)(2,1)S(1)}, bf16[2,32,768]{2,1,0:T(8,128)(2,1)S(1)}, u32[]{:S(2)}, u32[]{:S(2)}) %collective-permute-start.3) | collective-permute-done | bytes 98336 | tf_op jit(solution)/shard_map/ppermute | solution.py:254
  90.9 5.4 %collective-permute-start.4 = (bf16[1,32,768]{2,1,0:T(8,128)(2,1)S(1)}, bf16[1,32,768]{2,1,0:T(8,128)(2,1)S(1)}, u32[]{:S(2)}, u32[]{:S(2)}) collective-permute-start(bf16[1,32,768]{2,1,0:T(8,128)(2,1)S(1)} %get-tuple-element.34), channel_id=1, source_target_pairs={{0,256},{256,0},{1,257},{257,1},{2,258},{258,2},{3,259},{259,3},{4... | collective-permute-start | bytes 147464 | tf_op jit(solution)/shard_map/ppermute | solution.py:254
  96.3 2.1 %collective-permute-done.4.refs_1_ = bf16[1,32,768]{2,1,0:T(8,128)(2,1)S(1)} collective-permute-done((bf16[1,32,768]{2,1,0:T(8,128)(2,1)S(1)}, bf16[1,32,768]{2,1,0:T(8,128)(2,1)S(1)}, u32[]{:S(2)}, u32[]{:S(2)}) %collective-permute-start.4) | collective-permute-done | bytes 49184 | tf_op jit(solution)/shard_map/ppermute | solution.py:254
  98.4 0.6 shard_map.110
  99.0 0.0 all-to-all-done.1.back_ref
  99.0 0.0 copy-done.1
  99.0 1.1 %shard_map.105 = bf16[4,64,1024]{2,1,0:T(8,128)(2,1)} custom-call(bf16[4,128,64]{2,1,0:T(8,128)(2,1)S(1)} %copy-done.1, bf16[16,32,1024]{2,1,0:T(8,128)(2,1)S(1)} %all-to-all-done.1.back_ref), custom_call_target="tpu_custom_call" | custom-call | flops 134217728 | bytes 4194304 | tf_op jit(solution)/shard_map/pallas_call | solution.py:261
  (2 shorter events, 0.1 us)
Async XLA Ops:
  0.6 44.8 %copy-start.3 = (bf16[256,1024]{1,0:T(8,128)(2,1)S(1)}, bf16[256,1024]{1,0:T(8,128)(2,1)}, u32[]{:S(2)}) copy-start(bf16[256,1024]{1,0:T(8,128)(2,1)} %down_w_ref.1) | copy-start | bytes 1572868
  3.8 41.6 %copy-start.2 = (bf16[4,128,1024]{2,1,0:T(8,128)(2,1)S(1)}, bf16[4,128,1024]{2,1,0:T(8,128)(2,1)}, u32[]{:S(2)}) copy-start(bf16[4,128,1024]{2,1,0:T(8,128)(2,1)} %x_ref.1) | copy-start | bytes 3145732
  3.8 41.6 %copy-start.4 = (bf16[1024,256]{1,0:T(8,128)(2,1)S(1)}, bf16[1024,256]{1,0:T(8,128)(2,1)}, u32[]{:S(2)}) copy-start(bf16[1024,256]{1,0:T(8,128)(2,1)} %gate_w_ref.3) | copy-start | bytes 1572868
  3.8 41.6 %copy-start.5 = (bf16[1024,256]{1,0:T(8,128)(2,1)S(1)}, bf16[1024,256]{1,0:T(8,128)(2,1)}, u32[]{:S(2)}) copy-start(bf16[1024,256]{1,0:T(8,128)(2,1)} %up_w_ref.3) | copy-start | bytes 1572868
  50.2 1.0 copy-start
  51.2 47.8 %all-to-all-start.1 = ((bf16[16,32,1024]{2,1,0:T(8,128)(2,1)}), bf16[16,32,1024]{2,1,0:T(8,128)(2,1)S(1)}, u32[]{:S(2)}, u32[]{:S(2)}) async-start(bf16[16,32,1024]{2,1,0:T(8,128)(2,1)} %copy-done), calls=%async_computation.1 | async-start | bytes 2097152 | tf_op jit(solution)/shard_map/all_to_all | solution.py:251
  54.8 4.2 %collective-permute-start = (bf16[16,32,768]{2,1,0:T(8,128)(2,1)S(1)}, bf16[16,32,768]{2,1,0:T(8,128)(2,1)S(1)}, u32[]{:S(2)}, u32[]{:S(2)}) collective-permute-start(bf16[16,32,768]{2,1,0:T(8,128)(2,1)S(1)} %get-tuple-element.26), channel_id=1, source_target_pairs={{0,16},{16,0},{1,17},{17,1},{2,18},{18,2},{3,19},{19,3},{4,20},{20... | collective-permute-start | bytes 2359304 | tf_op jit(solution)/shard_map/ppermute | solution.py:254
  59.1 40.0 %copy-start.1 = (bf16[4,128,64]{2,1,0:T(8,128)(2,1)S(1)}, bf16[4,128,64]{2,1,0:T(8,128)(2,1)}, u32[]{:S(2)}) copy-start(bf16[4,128,64]{2,1,0:T(8,128)(2,1)} %get-tuple-element.21.pick_ref) | copy-start | bytes 196612
  59.1 13.2 %collective-permute-start.1 = (bf16[8,32,768]{2,1,0:T(8,128)(2,1)S(1)}, bf16[8,32,768]{2,1,0:T(8,128)(2,1)S(1)}, u32[]{:S(2)}, u32[]{:S(2)}) collective-permute-start(bf16[8,32,768]{2,1,0:T(8,128)(2,1)S(1)} %get-tuple-element.28), channel_id=1, source_target_pairs={{0,32},{32,0},{64,96},{96,64},{128,160},{160,128},{192,224},{224,1... | collective-permute-start | bytes 1179656 | tf_op jit(solution)/shard_map/ppermute | solution.py:254
  72.3 8.0 %collective-permute-start.2 = (bf16[4,32,768]{2,1,0:T(8,128)(2,1)S(1)}, bf16[4,32,768]{2,1,0:T(8,128)(2,1)S(1)}, u32[]{:S(2)}, u32[]{:S(2)}) collective-permute-start(bf16[4,32,768]{2,1,0:T(8,128)(2,1)S(1)} %get-tuple-element.30), channel_id=1, source_target_pairs={{0,224},{32,64},{64,32},{96,128},{128,96},{160,192},{192,160},{224... | collective-permute-start | bytes 589832 | tf_op jit(solution)/shard_map/ppermute | solution.py:254
  80.3 10.6 %collective-permute-start.3 = (bf16[2,32,768]{2,1,0:T(8,128)(2,1)S(1)}, bf16[2,32,768]{2,1,0:T(8,128)(2,1)S(1)}, u32[]{:S(2)}, u32[]{:S(2)}) collective-permute-start(bf16[2,32,768]{2,1,0:T(8,128)(2,1)S(1)} %get-tuple-element.32), channel_id=1, source_target_pairs={{0,96},{32,192},{64,160},{96,0},{128,224},{160,64},{192,32},{224,1... | collective-permute-start | bytes 294920 | tf_op jit(solution)/shard_map/ppermute | solution.py:254
  90.9 7.4 %collective-permute-start.4 = (bf16[1,32,768]{2,1,0:T(8,128)(2,1)S(1)}, bf16[1,32,768]{2,1,0:T(8,128)(2,1)S(1)}, u32[]{:S(2)}, u32[]{:S(2)}) collective-permute-start(bf16[1,32,768]{2,1,0:T(8,128)(2,1)S(1)} %get-tuple-element.34), channel_id=1, source_target_pairs={{0,256},{256,0},{1,257},{257,1},{2,258},{258,2},{3,259},{259,3},{4... | collective-permute-start | bytes 147464 | tf_op jit(solution)/shard_map/ppermute | solution.py:254

commit v4 on v3

--- a/solution.py
+++ b/solution.py
@@ -17,15 +17,19 @@
     return index ^ 1
 
 
-def after(index):
-    return (((index + 1) ^ 1) - 1) & 7
-
-
-def far(index):
-    return index ^ 3 ^ (((index ^ (index >> 1)) & 1) << 2)
-
-
-STAGES = (("core", near), ("y", near), ("y", after), ("y", far), ("zl", near))
+def plus(index):
+    return (index + 2) & 7
+
+
+def minus(index):
+    return (index + 6) & 7
+
+
+def cross(index):
+    return (index + 5 - 2 * (index & 1)) & 7
+
+
+TURNS = (cross, plus, minus)
 VMEM = pl.BlockSpec(memory_space=pltpu.VMEM)
 HBM = pl.BlockSpec(memory_space=pltpu.HBM)
 
@@ -53,11 +57,12 @@
     probs_hbm,
     grad_hbm,
     send_hbm,
-    pick_ref,
+    pick_hbm,
     ids_ref,
     probs_ref,
     grad_ref,
     send_ref,
+    pick_ref,
     sems,
     out_sems,
 ):
@@ -70,10 +75,10 @@
     for copy in copies:
         copy.start()
     micro, _, tokens = ids_ref.shape
-    holders = send_ref.shape[1]
-    rows = holders * CAPS
+    holders, _, width = send_ref.shape[1:]
+    rows = holders // 2 * CAPS
     row = lax.broadcasted_iota(jnp.int32, (rows, tokens), 0)
-    expert = row // (2 * CAPS)
+    expert = row // CAPS
     slot = (row % CAPS).astype(jnp.float32)
     earlier = (
         lax.broadcasted_iota(jnp.int32, (tokens, tokens), 0)
@@ -96,13 +101,18 @@
     copies[2].wait()
     puts = []
     for m in range(micro):
-        scaled = dot(weights[m], grad_ref[m], (1, 0))
-        send_ref[m] = scaled.astype(jnp.bfloat16).reshape(holders, CAPS, -1)
-        put = pltpu.make_async_copy(
-            send_ref.at[m], send_hbm.at[:, pl.ds(m * CAPS, CAPS), :], out_sems.at[m]
-        )
-        put.start()
-        puts.append(put)
+        scaled = dot(weights[m], grad_ref[m], (1, 0)).astype(jnp.bfloat16)
+        send_ref[m] = jnp.broadcast_to(
+            scaled.reshape(holders // 2, 1, CAPS, width), (holders // 2, 2, CAPS, width)
+        ).reshape(holders, CAPS, width)
+        puts.append(
+            pltpu.make_async_copy(
+                send_ref.at[m], send_hbm.at[:, pl.ds(m * CAPS, CAPS), :], out_sems.at[m]
+            )
+        )
+        puts[-1].start()
+    puts.append(pltpu.make_async_copy(pick_ref, pick_hbm, out_sems.at[micro]))
+    puts[-1].start()
     for put in puts:
         put.wait()
 
@@ -141,14 +151,13 @@
     for k, (left, right) in enumerate(terms):
         total = dot(left, right, (0, 0))
         all_ref[:, :, k * cols : (k + 1) * cols] = total.reshape(pieces, rows, cols)
+    plane, line, core = (lax.axis_index(axis) for axis in DP)
     for k in range(pieces // 2):
-        place = {axis: lax.axis_index(axis) for axis in DP}
-        for bit, (axis, partner) in enumerate(STAGES[1:]):
-            if k >> bit & 1:
-                place[axis] = partner(place[axis])
-        chip = (place["zl"] * lax.axis_size("y") + place["y"]) * 2
-        keep_ref[k] = all_ref[chip + place["core"]]
-        give_ref[k] = all_ref[chip + near(place["core"])].astype(jnp.bfloat16)
+        goal = near(line) if k & 1 else line
+        goal = TURNS[(k >> 2) - 1](goal) if k >> 2 else goal
+        chip = ((plane ^ (k >> 1 & 1)) * lax.axis_size("y") + goal) * 2
+        keep_ref[k] = all_ref[chip + core]
+        give_ref[k] = all_ref[chip + near(core)].astype(jnp.bfloat16)
 
 
 def slot_body(d_gate_ref, d_up_ref, gate_w_ref, up_w_ref, back_hbm, back_ref, sems):
@@ -178,11 +187,39 @@
         ).astype(jnp.bfloat16)
 
 
+def spread_body(keep_ref, other_ref, next_keep_ref, *give_refs):
+    for k in range(2):
+        turns = [
+            keep_ref[2 * t + k] + other_ref[2 * t + k].astype(jnp.float32)
+            for t in range(1 + len(give_refs))
+        ]
+        next_keep_ref[k] = turns[0]
+        for give_ref, turn in zip(give_refs, turns[1:]):
+            give_ref[k] = turn.astype(jnp.bfloat16)
+
+
+def gather_body(keep_ref, *refs):
+    *other_refs, next_keep_ref, give_ref = refs
+    total = keep_ref[...]
+    for other_ref in other_refs:
+        total = total + other_ref[...].astype(jnp.float32)
+    next_keep_ref[...] = total[:1]
+    give_ref[...] = total[1:].astype(jnp.bfloat16)
+
+
 def mix_body(pick_ref, back_ref, out_ref):
-    holders = back_ref.shape[0]
+    experts = back_ref.shape[0] // 2
     for m in range(pick_ref.shape[0]):
-        rows = back_ref[:, m * CAPS : (m + 1) * CAPS, :].reshape(holders * CAPS, -1)
-        out_ref[m] = dot(pick_ref[m], rows, (0, 0)).astype(jnp.bfloat16)
+        part = slice(m * CAPS, (m + 1) * CAPS)
+        halves = [
+            back_ref.at[pl.ds(0, 2 * experts), part][...]
+            .reshape(experts, 2, CAPS, -1)[:, h]
+            .reshape(experts * CAPS, -1)
+            for h in range(2)
+        ]
+        out_ref[m] = (
+            dot(pick_ref[m], halves[0], (0, 0)) + dot(pick_ref[m], halves[1], (0, 0))
+        ).astype(jnp.bfloat16)
 
 
 def total_body(factor, keep_ref, other_ref, *out_refs):
@@ -206,7 +243,7 @@
         route_body,
         (
             shape((holders, micro * CAPS, width), bf16),
-            shape((micro, holders * CAPS, tokens), bf16),
+            shape((micro, holders // 2 * CAPS, tokens), bf16),
         ),
         1 << 27,
         [HBM] * 3,
@@ -215,13 +252,15 @@
             pltpu.VMEM((micro, TOPK, tokens), bf16),
             pltpu.VMEM(grad_out.shape, bf16),
             pltpu.VMEM((micro, holders, CAPS, width), bf16),
+            pltpu.VMEM((micro, holders // 2 * CAPS, tokens), bf16),
             pltpu.SemaphoreType.DMA((3,)),
-            pltpu.SemaphoreType.DMA((micro,)),
+            pltpu.SemaphoreType.DMA((micro + 1,)),
         ],
-        1,
+        2,
         60,
     )(jnp.swapaxes(routes, 1, 2), jnp.swapaxes(route_probs, 1, 2), grad_out)
     got = lax.all_to_all(send, EXPERT, 0, 0, tiled=True)
+
     def lot(count):
         return count, rows, 3 * cols
 
@@ -249,15 +288,27 @@
         1,
     )(d_gate, d_up, w_gate, w_up)
     back = lax.all_to_all(back_send, EXPERT, 0, 0, tiled=True)
-    for stage, (axis, partner) in enumerate(STAGES):
-        goals = [(i, partner(i)) for i in range(lax.axis_size(axis))]
-        other = lax.ppermute(give, axis, goals)
-        if stage == len(STAGES) - 1:
-            break
-        half = lot(keep.shape[0] // 2)
-        keep, give = call(
-            halve_body, (shape(half, f32), shape(half, bf16)), 1 << 20, [VMEM] * 2
-        )(keep, other)
+
+    def swap(value, axis, partner):
+        return lax.ppermute(
+            value, axis, [(i, partner(i)) for i in range(lax.axis_size(axis))]
+        )
+
+    def small(body, count, sends, *values):
+        return call(
+            body,
+            (shape(lot(count), f32), *[shape(lot(count), bf16)] * sends),
+            1 << 20,
+            [VMEM] * len(values),
+        )(*values)
+
+    other = swap(give, "core", near)
+    keep, give = small(halve_body, pieces // 4, 1, keep, other)
+    other = swap(give, "y", near)
+    keep, *gives = small(spread_body, 2, len(TURNS), keep, other)
+    others = [swap(give, "y", turn) for turn, give in zip(TURNS, gives)]
+    keep, give = small(gather_body, 1, 1, keep, *others)
+    other = swap(give, "zl", near)
     (grad_in,) = call(
         mix_body, (shape((micro, tokens, width), bf16),), 1 << 27, [VMEM] * 2
     )(pick, back)

time: 101 us -> 100 us (0.990)
  the two profiles are of different devices: /device:TPU:42 before, /device:TPU:50 now
where the time goes in v4:
time: 100 us; the launch traced here: 99.8 us
  blocking collectives  41.6 us (42%)
  starting transfers between devices  24.1 us (24%)
  waiting for transfers between devices  23.1 us (23%)
  Pallas kernels  9.2 us (9%)
  local copies, waits for them, and re-layouts  1 us (1%)
    all_to_all x1, blocking collectives, per_device(): got = lax.all_to_all(send, EXPERT, 0, 0, tiled=True)  41.6 us
    ppermute x6, waiting for transfers between devices, swap(): lax.ppermute(value, axis, [(i, partner(i)) for i in range(lax.axis_size(a...  23.1 us
    ppermute x6, starting transfers between devices, swap(): lax.ppermute(value, axis, [(i, partner(i)) for i in range(lax.axis_size(a...  20.5 us
    all_to_all x1, starting transfers between devices, per_device(): back = lax.all_to_all(back_send, EXPERT, 0, 0, tiled=True)  3.55 us
    pallas_call x1, Pallas kernels, per_device(): call(weight_body, (shape((micro * slots, cols), bf16), shape((micro * slo...  2.68 us
    pallas_call x1, Pallas kernels, per_device(): call(route_body, (shape((holders, micro * CAPS, width), bf16), shape((mic...  2.37 us
    pallas_call x1, Pallas kernels, per_device(): call(slot_body, (shape((holders, micro * CAPS, width), bf16),), 1 << 30,...  2.03 us
  transfers between devices with their start and end apart: 7, of which 5 were waited for; matrix products, arithmetic and copies ran while one was open for 0% of the time, Pallas kernels for 1%

profile of v4, /device:TPU:50, one launch (start us, length us, event | category | flops | bytes accessed | tf_op | source)
XLA Modules:
  0.0 99.8 jit_solution(7890302367917977111)
XLA Ops:
  0.6 0.0 copy-start.3
  0.6 2.4 %shard_map.102 = (bf16[16,32,1024]{2,1,0:T(8,128)(2,1)}, bf16[4,64,64]{2,1,0:T(8,128)(2,1)}) custom-call(s32[4,8,64]{2,1,0:T(8,128)} %bitcast.2, bf16[4,8,64]{2,1,0:T(8,128)(2,1)} %bitcast.3, bf16[4,64,1024]{2,1,0:T(8,128)(2,1)} %grad_hbm.1), custom_call_target="tpu_custom_call" | custom-call | flops 134217728 | bytes 4194304 | tf_op jit(solution)/shard_map/pallas_call | solution.py:242
  3.0 0.0 copy-start.2
  3.0 0.0 copy-start.4
  3.0 0.0 copy-start.5
  3.1 41.6 %all_to_all.10.got_ref = bf16[16,32,1024]{2,1,0:T(8,128)(2,1)S(1)} all-to-all(bf16[16,32,1024]{2,1,0:T(8,128)(2,1)} %get-tuple-element.22), channel_id=1, replica_groups=mesh['zl'=2,'y'=8,'core'=2,'x'=4,'zq'=2,'zp'=2] {'x','zq','zp'}, dimensions={0} | all-to-all | bytes 2097152 | tf_op jit(solution)/shard_map/all_to_all | solution.py:262
  44.7 0.0 copy-done.3
  44.7 0.0 copy-done.2
  44.7 0.0 copy-done.4
  44.7 0.0 copy-done.5
  44.7 2.7 %shard_map.103 = (bf16[512,256]{1,0:T(8,128)(2,1)S(1)}, bf16[512,256]{1,0:T(8,128)(2,1)S(1)}, f32[16,32,768]{2,1,0:T(8,128)S(1)}, bf16[16,32,768]{2,1,0:T(8,128)(2,1)S(1)}) custom-call(bf16[16,32,1024]{2,1,0:T(8,128)(2,1)S(1)} %all_to_all.10.got_ref, bf16[4,128,1024]{2,1,0:T(8,128)(2,1)S(1)} %copy-done.2, bf16[1024,256]{1,0:T(8,128)(2,1)S(1)} %copy-done.4, ...), custom_call_target="tpu_custom_call" | custom-call | flops 2147483648 | bytes 4194304 | tf_op jit(solution)/shard_map/pallas_call | solution.py:267
  47.4 2.0 %shard_map.104 = bf16[16,32,1024]{2,1,0:T(8,128)(2,1)S(1)} custom-call(bf16[512,256]{1,0:T(8,128)(2,1)S(1)} %get-tuple-element.23.d_gate_ref, bf16[512,256]{1,0:T(8,128)(2,1)S(1)} %get-tuple-element.24.d_up_ref, bf16[1024,256]{1,0:T(8,128)(2,1)S(1)} %copy-done.4, bf16[1024,256]{1,0:T(8,128)(2,1)S(1)} %copy-done.5), custom_call_target="tpu_custom_call" | custom-call | flops 1073741824 | bytes 4194304 | tf_op jit(solution)/shard_map/pallas_call | solution.py:279
  49.4 0.0 copy-start
  49.4 1.0 copy-done
  50.4 3.5 %all-to-all-start.1 = ((bf16[16,32,1024]{2,1,0:T(8,128)(2,1)}), bf16[16,32,1024]{2,1,0:T(8,128)(2,1)S(1)}, u32[]{:S(2)}, u32[]{:S(2)}) async-start(bf16[16,32,1024]{2,1,0:T(8,128)(2,1)} %copy-done), calls=%async_computation.1 | async-start | bytes 2097152 | tf_op jit(solution)/shard_map/all_to_all | solution.py:290
  54.0 1.9 %collective-permute-start = (bf16[16,32,768]{2,1,0:T(8,128)(2,1)S(1)}, bf16[16,32,768]{2,1,0:T(8,128)(2,1)S(1)}, u32[]{:S(2)}, u32[]{:S(2)}) collective-permute-start(bf16[16,32,768]{2,1,0:T(8,128)(2,1)S(1)} %get-tuple-element.26), channel_id=1, source_target_pairs={{0,16},{16,0},{1,17},{17,1},{2,18},{18,2},{3,19},{19,3},{4,20},{20... | collective-permute-start | bytes 2359304 | tf_op jit(solution)/shard_map/ppermute | solution.py:293
  55.9 2.3 %collective-permute-done.other_ref = bf16[16,32,768]{2,1,0:T(8,128)(2,1)S(1)} collective-permute-done((bf16[16,32,768]{2,1,0:T(8,128)(2,1)S(1)}, bf16[16,32,768]{2,1,0:T(8,128)(2,1)S(1)}, u32[]{:S(2)}, u32[]{:S(2)}) %collective-permute-start) | collective-permute-done | bytes 786464 | tf_op jit(solution)/shard_map/ppermute | solution.py:293
  58.1 0.0 copy-start.1
  58.1 0.1 shard_map.106
  58.3 2.6 %collective-permute-start.1 = (bf16[8,32,768]{2,1,0:T(8,128)(2,1)S(1)}, bf16[8,32,768]{2,1,0:T(8,128)(2,1)S(1)}, u32[]{:S(2)}, u32[]{:S(2)}) collective-permute-start(bf16[8,32,768]{2,1,0:T(8,128)(2,1)S(1)} %get-tuple-element.28), channel_id=1, source_target_pairs={{0,32},{32,0},{64,96},{96,64},{128,160},{160,128},{192,224},{224,1... | collective-permute-start | bytes 1179656 | tf_op jit(solution)/shard_map/ppermute | solution.py:293
  60.9 10.4 %collective-permute-done.1.other_ref = bf16[8,32,768]{2,1,0:T(8,128)(2,1)S(1)} collective-permute-done((bf16[8,32,768]{2,1,0:T(8,128)(2,1)S(1)}, bf16[8,32,768]{2,1,0:T(8,128)(2,1)S(1)}, u32[]{:S(2)}, u32[]{:S(2)}) %collective-permute-start.1) | collective-permute-done | bytes 393248 | tf_op jit(solution)/shard_map/ppermute | solution.py:293
  71.3 0.1 shard_map.107
  71.4 3.9 %collective-permute-start.2 = (bf16[2,32,768]{2,1,0:T(8,128)(2,1)S(1)}, bf16[2,32,768]{2,1,0:T(8,128)(2,1)S(1)}, u32[]{:S(2)}, u32[]{:S(2)}) collective-permute-start(bf16[2,32,768]{2,1,0:T(8,128)(2,1)S(1)} %get-tuple-element.30), channel_id=1, source_target_pairs={{0,160},{32,128},{64,224},{96,192},{128,32},{160,0},{192,96},{224,... | collective-permute-start | bytes 294920 | tf_op jit(solution)/shard_map/ppermute | solution.py:293
  75.3 4.8 %collective-permute-start.3 = (bf16[2,32,768]{2,1,0:T(8,128)(2,1)S(1)}, bf16[2,32,768]{2,1,0:T(8,128)(2,1)S(1)}, u32[]{:S(2)}, u32[]{:S(2)}) collective-permute-start(bf16[2,32,768]{2,1,0:T(8,128)(2,1)S(1)} %get-tuple-element.31), channel_id=1, source_target_pairs={{0,64},{32,96},{64,128},{96,160},{128,192},{160,224},{192,0},{224,... | collective-permute-start | bytes 294920 | tf_op jit(solution)/shard_map/ppermute | solution.py:293
  80.1 1.9 %collective-permute-start.4 = (bf16[2,32,768]{2,1,0:T(8,128)(2,1)S(1)}, bf16[2,32,768]{2,1,0:T(8,128)(2,1)S(1)}, u32[]{:S(2)}, u32[]{:S(2)}) collective-permute-start(bf16[2,32,768]{2,1,0:T(8,128)(2,1)S(1)} %get-tuple-element.32), channel_id=1, source_target_pairs={{0,192},{32,224},{64,0},{96,32},{128,64},{160,96},{192,128},{224,1... | collective-permute-start | bytes 294920 | tf_op jit(solution)/shard_map/ppermute | solution.py:293
  82.1 3.7 %collective-permute-done.2.refs_0_ = bf16[2,32,768]{2,1,0:T(8,128)(2,1)S(1)} collective-permute-done((bf16[2,32,768]{2,1,0:T(8,128)(2,1)S(1)}, bf16[2,32,768]{2,1,0:T(8,128)(2,1)S(1)}, u32[]{:S(2)}, u32[]{:S(2)}) %collective-permute-start.2) | collective-permute-done | bytes 98336 | tf_op jit(solution)/shard_map/ppermute | solution.py:293
  85.8 0.0 collective-permute-done.3.refs_1_
  85.8 4.7 %collective-permute-done.4.refs_2_ = bf16[2,32,768]{2,1,0:T(8,128)(2,1)S(1)} collective-permute-done((bf16[2,32,768]{2,1,0:T(8,128)(2,1)S(1)}, bf16[2,32,768]{2,1,0:T(8,128)(2,1)S(1)}, u32[]{:S(2)}, u32[]{:S(2)}) %collective-permute-start.4) | collective-permute-done | bytes 98336 | tf_op jit(solution)/shard_map/ppermute | solution.py:293
  90.5 5.4 %collective-permute-start.5 = (bf16[1,32,768]{2,1,0:T(8,128)(2,1)S(1)}, bf16[1,32,768]{2,1,0:T(8,128)(2,1)S(1)}, u32[]{:S(2)}, u32[]{:S(2)}) collective-permute-start(bf16[1,32,768]{2,1,0:T(8,128)(2,1)S(1)} %get-tuple-element.34), channel_id=1, source_target_pairs={{0,256},{256,0},{1,257},{257,1},{2,258},{258,2},{3,259},{259,3},{4... | collective-permute-start | bytes 147464 | tf_op jit(solution)/shard_map/ppermute | solution.py:293
  95.9 2.1 %collective-permute-done.5.refs_1_ = bf16[1,32,768]{2,1,0:T(8,128)(2,1)S(1)} collective-permute-done((bf16[1,32,768]{2,1,0:T(8,128)(2,1)S(1)}, bf16[1,32,768]{2,1,0:T(8,128)(2,1)S(1)}, u32[]{:S(2)}, u32[]{:S(2)}) %collective-permute-start.5) | collective-permute-done | bytes 49184 | tf_op jit(solution)/shard_map/ppermute | solution.py:293
  97.9 0.6 shard_map.109
  98.6 0.0 all-to-all-done.1.back_ref
  98.6 0.0 copy-done.1
  98.6 1.2 %shard_map.105 = bf16[4,64,1024]{2,1,0:T(8,128)(2,1)} custom-call(bf16[4,64,64]{2,1,0:T(8,128)(2,1)S(1)} %copy-done.1, bf16[16,32,1024]{2,1,0:T(8,128)(2,1)S(1)} %all-to-all-done.1.back_ref), custom_call_target="tpu_custom_call" | custom-call | flops 134217728 | bytes 4194304 | tf_op jit(solution)/shard_map/pallas_call | solution.py:312
  (1 shorter events, 0.0 us)
Async XLA Ops:
  0.6 44.0 %copy-start.3 = (bf16[256,1024]{1,0:T(8,128)(2,1)S(1)}, bf16[256,1024]{1,0:T(8,128)(2,1)}, u32[]{:S(2)}) copy-start(bf16[256,1024]{1,0:T(8,128)(2,1)} %down_w_ref.1) | copy-start | bytes 1572868
  3.0 41.7 %copy-start.2 = (bf16[4,128,1024]{2,1,0:T(8,128)(2,1)S(1)}, bf16[4,128,1024]{2,1,0:T(8,128)(2,1)}, u32[]{:S(2)}) copy-start(bf16[4,128,1024]{2,1,0:T(8,128)(2,1)} %x_ref.1) | copy-start | bytes 3145732
  3.0 41.6 %copy-start.4 = (bf16[1024,256]{1,0:T(8,128)(2,1)S(1)}, bf16[1024,256]{1,0:T(8,128)(2,1)}, u32[]{:S(2)}) copy-start(bf16[1024,256]{1,0:T(8,128)(2,1)} %gate_w_ref.3) | copy-start | bytes 1572868
  3.0 41.6 %copy-start.5 = (bf16[1024,256]{1,0:T(8,128)(2,1)S(1)}, bf16[1024,256]{1,0:T(8,128)(2,1)}, u32[]{:S(2)}) copy-start(bf16[1024,256]{1,0:T(8,128)(2,1)} %up_w_ref.3) | copy-start | bytes 1572868
  49.4 1.0 copy-start
  50.4 48.2 %all-to-all-start.1 = ((bf16[16,32,1024]{2,1,0:T(8,128)(2,1)}), bf16[16,32,1024]{2,1,0:T(8,128)(2,1)S(1)}, u32[]{:S(2)}, u32[]{:S(2)}) async-start(bf16[16,32,1024]{2,1,0:T(8,128)(2,1)} %copy-done), calls=%async_computation.1 | async-start | bytes 2097152 | tf_op jit(solution)/shard_map/all_to_all | solution.py:290
  54.0 4.2 %collective-permute-start = (bf16[16,32,768]{2,1,0:T(8,128)(2,1)S(1)}, bf16[16,32,768]{2,1,0:T(8,128)(2,1)S(1)}, u32[]{:S(2)}, u32[]{:S(2)}) collective-permute-start(bf16[16,32,768]{2,1,0:T(8,128)(2,1)S(1)} %get-tuple-element.26), channel_id=1, source_target_pairs={{0,16},{16,0},{1,17},{17,1},{2,18},{18,2},{3,19},{19,3},{4,20},{20... | collective-permute-start | bytes 2359304 | tf_op jit(solution)/shard_map/ppermute | solution.py:293
  58.1 40.4 %copy-start.1 = (bf16[4,64,64]{2,1,0:T(8,128)(2,1)S(1)}, bf16[4,64,64]{2,1,0:T(8,128)(2,1)}, u32[]{:S(2)}) copy-start(bf16[4,64,64]{2,1,0:T(8,128)(2,1)} %get-tuple-element.21.pick_ref) | copy-start | bytes 98308
  58.3 13.1 %collective-permute-start.1 = (bf16[8,32,768]{2,1,0:T(8,128)(2,1)S(1)}, bf16[8,32,768]{2,1,0:T(8,128)(2,1)S(1)}, u32[]{:S(2)}, u32[]{:S(2)}) collective-permute-start(bf16[8,32,768]{2,1,0:T(8,128)(2,1)S(1)} %get-tuple-element.28), channel_id=1, source_target_pairs={{0,32},{32,0},{64,96},{96,64},{128,160},{160,128},{192,224},{224,1... | collective-permute-start | bytes 1179656 | tf_op jit(solution)/shard_map/ppermute | solution.py:293
  71.4 14.4 %collective-permute-start.2 = (bf16[2,32,768]{2,1,0:T(8,128)(2,1)S(1)}, bf16[2,32,768]{2,1,0:T(8,128)(2,1)S(1)}, u32[]{:S(2)}, u32[]{:S(2)}) collective-permute-start(bf16[2,32,768]{2,1,0:T(8,128)(2,1)S(1)} %get-tuple-element.30), channel_id=1, source_target_pairs={{0,160},{32,128},{64,224},{96,192},{128,32},{160,0},{192,96},{224,... | collective-permute-start | bytes 294920 | tf_op jit(solution)/shard_map/ppermute | solution.py:293
  75.3 10.5 %collective-permute-start.3 = (bf16[2,32,768]{2,1,0:T(8,128)(2,1)S(1)}, bf16[2,32,768]{2,1,0:T(8,128)(2,1)S(1)}, u32[]{:S(2)}, u32[]{:S(2)}) collective-permute-start(bf16[2,32,768]{2,1,0:T(8,128)(2,1)S(1)} %get-tuple-element.31), channel_id=1, source_target_pairs={{0,64},{32,96},{64,128},{96,160},{128,192},{160,224},{192,0},{224,... | collective-permute-start | bytes 294920 | tf_op jit(solution)/shard_map/ppermute | solution.py:293
  80.1 10.3 %collective-permute-start.4 = (bf16[2,32,768]{2,1,0:T(8,128)(2,1)S(1)}, bf16[2,32,768]{2,1,0:T(8,128)(2,1)S(1)}, u32[]{:S(2)}, u32[]{:S(2)}) collective-permute-start(bf16[2,32,768]{2,1,0:T(8,128)(2,1)S(1)} %get-tuple-element.32), channel_id=1, source_target_pairs={{0,192},{32,224},{64,0},{96,32},{128,64},{160,96},{192,128},{224,1... | collective-permute-start | bytes 294920 | tf_op jit(solution)/shard_map/ppermute | solution.py:293
  90.5 7.4 %collective-permute-start.5 = (bf16[1,32,768]{2,1,0:T(8,128)(2,1)S(1)}, bf16[1,32,768]{2,1,0:T(8,128)(2,1)S(1)}, u32[]{:S(2)}, u32[]{:S(2)}) collective-permute-start(bf16[1,32,768]{2,1,0:T(8,128)(2,1)S(1)} %get-tuple-element.34), channel_id=1, source_target_pairs={{0,256},{256,0},{1,257},{257,1},{2,258},{258,2},{3,259},{259,3},{4... | collective-permute-start | bytes 147464 | tf_op jit(solution)/shard_map/ppermute | solution.py:293

commit v5 on v4

--- a/solution.py
+++ b/solution.py
@@ -30,6 +30,7 @@
 
 
 TURNS = (cross, plus, minus)
+PARTS = 4
 VMEM = pl.BlockSpec(memory_space=pltpu.VMEM)
 HBM = pl.BlockSpec(memory_space=pltpu.HBM)
 
@@ -123,8 +124,7 @@
     gate_w_ref,
     up_w_ref,
     down_w_ref,
-    d_gate_ref,
-    d_up_ref,
+    d_both_ref,
     keep_ref,
     give_ref,
     got_all_ref,
@@ -145,12 +145,12 @@
     hidden = (activated * up).astype(jnp.bfloat16)
     to_gate = up * sigmoid * (1.0 + gate * (1.0 - sigmoid))
     d_hidden = dot(got_all_ref[...], down_w_ref[...], (1, 1))
-    d_gate_ref[...] = (d_hidden * to_gate).astype(jnp.bfloat16)
-    d_up_ref[...] = (d_hidden * activated).astype(jnp.bfloat16)
-    terms = ((x, d_gate_ref[...]), (x, d_up_ref[...]), (got_all_ref[...], hidden))
-    for k, (left, right) in enumerate(terms):
-        total = dot(left, right, (0, 0))
-        all_ref[:, :, k * cols : (k + 1) * cols] = total.reshape(pieces, rows, cols)
+    d_both_ref[:, :cols] = (d_hidden * to_gate).astype(jnp.bfloat16)
+    d_both_ref[:, cols:] = (d_hidden * activated).astype(jnp.bfloat16)
+    total = dot(x, d_both_ref[...], (0, 0))
+    all_ref[:, :, : 2 * cols] = total.reshape(pieces, rows, 2 * cols)
+    total = dot(got_all_ref[...], hidden, (0, 0))
+    all_ref[:, :, 2 * cols :] = total.reshape(pieces, rows, cols)
     plane, line, core = (lax.axis_index(axis) for axis in DP)
     for k in range(pieces // 2):
         goal = near(line) if k & 1 else line
@@ -160,21 +160,24 @@
         give_ref[k] = all_ref[chip + near(core)].astype(jnp.bfloat16)
 
 
-def slot_body(d_gate_ref, d_up_ref, gate_w_ref, up_w_ref, back_hbm, back_ref, sems):
-    micro, holders, _, width = back_ref.shape
-    slots = holders * CAPS
+def slot_body(d_both_ref, gate_w_ref, up_w_ref, back_hbm, back_ref, sems):
+    parts, micro, holders, _, width = back_ref.shape
+    cols = gate_w_ref.shape[1]
     puts = []
-    for m in range(micro):
-        rows = slice(m * slots, (m + 1) * slots)
-        back = dot(d_gate_ref[rows], gate_w_ref[...], (1, 1)) + dot(
-            d_up_ref[rows], up_w_ref[...], (1, 1)
+    for n in range(parts):
+        span = pl.ds(n * width, width)
+        back = dot(d_both_ref[:, :cols], gate_w_ref[span, :], (1, 1)) + dot(
+            d_both_ref[:, cols:], up_w_ref[span, :], (1, 1)
         )
-        back_ref[m] = back.astype(jnp.bfloat16).reshape(holders, CAPS, width)
-        put = pltpu.make_async_copy(
-            back_ref.at[m], back_hbm.at[:, pl.ds(m * CAPS, CAPS), :], sems.at[m]
-        )
-        put.start()
-        puts.append(put)
+        back_ref[n] = back.astype(jnp.bfloat16).reshape(micro, holders, CAPS, width)
+        for m in range(micro):
+            put = pltpu.make_async_copy(
+                back_ref.at[n, m],
+                back_hbm.at[:, pl.ds(m * CAPS, CAPS), span],
+                sems.at[n * micro + m],
+            )
+            put.start()
+            puts.append(put)
     for put in puts:
         put.wait()
 
@@ -264,11 +267,10 @@
     def lot(count):
         return count, rows, 3 * cols
 
-    d_gate, d_up, keep, give = call(
+    d_both, keep, give = call(
         weight_body,
         (
-            shape((micro * slots, cols), bf16),
-            shape((micro * slots, cols), bf16),
+            shape((micro * slots, 2 * cols), bf16),
             shape(lot(pieces // 2), f32),
             shape(lot(pieces // 2), bf16),
         ),
@@ -280,13 +282,13 @@
         slot_body,
         (shape((holders, micro * CAPS, width), bf16),),
         1 << 30,
-        [VMEM] * 4,
+        [VMEM] * 3,
         [
-            pltpu.VMEM((micro, holders, CAPS, width), bf16),
-            pltpu.SemaphoreType.DMA((micro,)),
+            pltpu.VMEM((PARTS, micro, holders, CAPS, width // PARTS), bf16),
+            pltpu.SemaphoreType.DMA((PARTS * micro,)),
         ],
         1,
-    )(d_gate, d_up, w_gate, w_up)
+    )(d_both, w_gate, w_up)
     back = lax.all_to_all(back_send, EXPERT, 0, 0, tiled=True)
 
     def swap(value, axis, partner):

time: 100 us -> 100 us (level)
  no operation moved by 1% of the time
where the time goes in v5:
time: 100 us; the launch traced here: 99.9 us
  blocking collectives  41.6 us (42%)
  starting transfers between devices  24.1 us (24%)
  waiting for transfers between devices  23.1 us (23%)
  Pallas kernels  9.31 us (9%)
  local copies, waits for them, and re-layouts  1 us (1%)
    all_to_all x1, blocking collectives, per_device(): got = lax.all_to_all(send, EXPERT, 0, 0, tiled=True)  41.6 us
    ppermute x6, waiting for transfers between devices, swap(): lax.ppermute(value, axis, [(i, partner(i)) for i in range(lax.axis_size(a...  23.1 us
    ppermute x6, starting transfers between devices, swap(): lax.ppermute(value, axis, [(i, partner(i)) for i in range(lax.axis_size(a...  20.5 us
    all_to_all x1, starting transfers between devices, per_device(): back = lax.all_to_all(back_send, EXPERT, 0, 0, tiled=True)  3.55 us
    pallas_call x1, Pallas kernels, per_device(): call(weight_body, (shape((micro * slots, 2 * cols), bf16), shape(lot(piec...  2.67 us
    pallas_call x1, Pallas kernels, per_device(): call(route_body, (shape((holders, micro * CAPS, width), bf16), shape((mic...  2.37 us
    pallas_call x1, Pallas kernels, per_device(): call(slot_body, (shape((holders, micro * CAPS, width), bf16),), 1 << 30,...  2.13 us
  transfers between devices with their start and end apart: 7, of which 5 were waited for; matrix products, arithmetic and copies ran while one was open for 0% of the time, Pallas kernels for 1%

profile of v5, /device:TPU:50, one launch (start us, length us, event | category | flops | bytes accessed | tf_op | source)
XLA Modules:
  0.0 99.9 jit_solution(5006217610960510737)
XLA Ops:
  0.6 0.0 copy-start.3
  0.6 2.4 %shard_map.102 = (bf16[16,32,1024]{2,1,0:T(8,128)(2,1)}, bf16[4,64,64]{2,1,0:T(8,128)(2,1)}) custom-call(s32[4,8,64]{2,1,0:T(8,128)} %bitcast.2, bf16[4,8,64]{2,1,0:T(8,128)(2,1)} %bitcast.3, bf16[4,64,1024]{2,1,0:T(8,128)(2,1)} %grad_hbm.1), custom_call_target="tpu_custom_call" | custom-call | flops 134217728 | bytes 4194304 | tf_op jit(solution)/shard_map/pallas_call | solution.py:245
  3.0 0.0 copy-start.2
  3.0 0.0 copy-start.4
  3.0 0.0 copy-start.5
  3.1 41.6 %all_to_all.10.got_ref = bf16[16,32,1024]{2,1,0:T(8,128)(2,1)S(1)} all-to-all(bf16[16,32,1024]{2,1,0:T(8,128)(2,1)} %get-tuple-element.21), channel_id=1, replica_groups=mesh['zl'=2,'y'=8,'core'=2,'x'=4,'zq'=2,'zp'=2] {'x','zq','zp'}, dimensions={0} | all-to-all | bytes 2097152 | tf_op jit(solution)/shard_map/all_to_all | solution.py:265
  44.7 0.0 copy-done.3
  44.7 0.0 copy-done.2
  44.7 0.0 copy-done.4
  44.7 0.0 copy-done.5
  44.7 2.7 %shard_map.103 = (bf16[512,512]{1,0:T(8,128)(2,1)S(1)}, f32[16,32,768]{2,1,0:T(8,128)S(1)}, bf16[16,32,768]{2,1,0:T(8,128)(2,1)S(1)}) custom-call(bf16[16,32,1024]{2,1,0:T(8,128)(2,1)S(1)} %all_to_all.10.got_ref, bf16[4,128,1024]{2,1,0:T(8,128)(2,1)S(1)} %copy-done.2, bf16[1024,256]{1,0:T(8,128)(2,1)S(1)} %copy-done.4, bf16[1024,256]{1,0:T(8,128)(2,1)S(1)} %copy-done.5, ...), custom_call_target="tpu_custom_call" | custom-call | flops 2147483648 | bytes 4194304 | tf_op jit(solution)/shard_map/pallas_call | solution.py:270
  47.4 2.1 %shard_map.104 = bf16[16,32,1024]{2,1,0:T(8,128)(2,1)S(1)} custom-call(bf16[512,512]{1,0:T(8,128)(2,1)S(1)} %get-tuple-element.22.d_both_ref, bf16[1024,256]{1,0:T(8,128)(2,1)S(1)} %copy-done.4, bf16[1024,256]{1,0:T(8,128)(2,1)S(1)} %copy-done.5), custom_call_target="tpu_custom_call" | custom-call | flops 1073741824 | bytes 4194304 | tf_op jit(solution)/shard_map/pallas_call | solution.py:281
  49.5 0.0 copy-start
  49.5 1.0 copy-done
  50.5 3.5 %all-to-all-start.1 = ((bf16[16,32,1024]{2,1,0:T(8,128)(2,1)}), bf16[16,32,1024]{2,1,0:T(8,128)(2,1)S(1)}, u32[]{:S(2)}, u32[]{:S(2)}) async-start(bf16[16,32,1024]{2,1,0:T(8,128)(2,1)} %copy-done), calls=%async_computation.1 | async-start | bytes 2097152 | tf_op jit(solution)/shard_map/all_to_all | solution.py:292
  54.0 1.9 %collective-permute-start = (bf16[16,32,768]{2,1,0:T(8,128)(2,1)S(1)}, bf16[16,32,768]{2,1,0:T(8,128)(2,1)S(1)}, u32[]{:S(2)}, u32[]{:S(2)}) collective-permute-start(bf16[16,32,768]{2,1,0:T(8,128)(2,1)S(1)} %get-tuple-element.24), channel_id=1, source_target_pairs={{0,16},{16,0},{1,17},{17,1},{2,18},{18,2},{3,19},{19,3},{4,20},{20... | collective-permute-start | bytes 2359304 | tf_op jit(solution)/shard_map/ppermute | solution.py:295
  56.0 2.3 %collective-permute-done.other_ref = bf16[16,32,768]{2,1,0:T(8,128)(2,1)S(1)} collective-permute-done((bf16[16,32,768]{2,1,0:T(8,128)(2,1)S(1)}, bf16[16,32,768]{2,1,0:T(8,128)(2,1)S(1)}, u32[]{:S(2)}, u32[]{:S(2)}) %collective-permute-start) | collective-permute-done | bytes 786464 | tf_op jit(solution)/shard_map/ppermute | solution.py:295
  58.2 0.0 copy-start.1
  58.2 0.1 shard_map.106
  58.4 2.6 %collective-permute-start.1 = (bf16[8,32,768]{2,1,0:T(8,128)(2,1)S(1)}, bf16[8,32,768]{2,1,0:T(8,128)(2,1)S(1)}, u32[]{:S(2)}, u32[]{:S(2)}) collective-permute-start(bf16[8,32,768]{2,1,0:T(8,128)(2,1)S(1)} %get-tuple-element.26), channel_id=1, source_target_pairs={{0,32},{32,0},{64,96},{96,64},{128,160},{160,128},{192,224},{224,1... | collective-permute-start | bytes 1179656 | tf_op jit(solution)/shard_map/ppermute | solution.py:295
  61.0 10.5 %collective-permute-done.1.other_ref = bf16[8,32,768]{2,1,0:T(8,128)(2,1)S(1)} collective-permute-done((bf16[8,32,768]{2,1,0:T(8,128)(2,1)S(1)}, bf16[8,32,768]{2,1,0:T(8,128)(2,1)S(1)}, u32[]{:S(2)}, u32[]{:S(2)}) %collective-permute-start.1) | collective-permute-done | bytes 393248 | tf_op jit(solution)/shard_map/ppermute | solution.py:295
  71.4 0.1 shard_map.107
  71.5 3.9 %collective-permute-start.2 = (bf16[2,32,768]{2,1,0:T(8,128)(2,1)S(1)}, bf16[2,32,768]{2,1,0:T(8,128)(2,1)S(1)}, u32[]{:S(2)}, u32[]{:S(2)}) collective-permute-start(bf16[2,32,768]{2,1,0:T(8,128)(2,1)S(1)} %get-tuple-element.28), channel_id=1, source_target_pairs={{0,160},{32,128},{64,224},{96,192},{128,32},{160,0},{192,96},{224,... | collective-permute-start | bytes 294920 | tf_op jit(solution)/shard_map/ppermute | solution.py:295
  75.4 4.8 %collective-permute-start.3 = (bf16[2,32,768]{2,1,0:T(8,128)(2,1)S(1)}, bf16[2,32,768]{2,1,0:T(8,128)(2,1)S(1)}, u32[]{:S(2)}, u32[]{:S(2)}) collective-permute-start(bf16[2,32,768]{2,1,0:T(8,128)(2,1)S(1)} %get-tuple-element.29), channel_id=1, source_target_pairs={{0,64},{32,96},{64,128},{96,160},{128,192},{160,224},{192,0},{224,... | collective-permute-start | bytes 294920 | tf_op jit(solution)/shard_map/ppermute | solution.py:295
  80.2 1.9 %collective-permute-start.4 = (bf16[2,32,768]{2,1,0:T(8,128)(2,1)S(1)}, bf16[2,32,768]{2,1,0:T(8,128)(2,1)S(1)}, u32[]{:S(2)}, u32[]{:S(2)}) collective-permute-start(bf16[2,32,768]{2,1,0:T(8,128)(2,1)S(1)} %get-tuple-element.30), channel_id=1, source_target_pairs={{0,192},{32,224},{64,0},{96,32},{128,64},{160,96},{192,128},{224,1... | collective-permute-start | bytes 294920 | tf_op jit(solution)/shard_map/ppermute | solution.py:295
  82.2 3.7 %collective-permute-done.2.refs_0_ = bf16[2,32,768]{2,1,0:T(8,128)(2,1)S(1)} collective-permute-done((bf16[2,32,768]{2,1,0:T(8,128)(2,1)S(1)}, bf16[2,32,768]{2,1,0:T(8,128)(2,1)S(1)}, u32[]{:S(2)}, u32[]{:S(2)}) %collective-permute-start.2) | collective-permute-done | bytes 98336 | tf_op jit(solution)/shard_map/ppermute | solution.py:295
  85.9 0.0 collective-permute-done.3.refs_1_
  85.9 4.7 %collective-permute-done.4.refs_2_ = bf16[2,32,768]{2,1,0:T(8,128)(2,1)S(1)} collective-permute-done((bf16[2,32,768]{2,1,0:T(8,128)(2,1)S(1)}, bf16[2,32,768]{2,1,0:T(8,128)(2,1)S(1)}, u32[]{:S(2)}, u32[]{:S(2)}) %collective-permute-start.4) | collective-permute-done | bytes 98336 | tf_op jit(solution)/shard_map/ppermute | solution.py:295
  90.6 5.4 %collective-permute-start.5 = (bf16[1,32,768]{2,1,0:T(8,128)(2,1)S(1)}, bf16[1,32,768]{2,1,0:T(8,128)(2,1)S(1)}, u32[]{:S(2)}, u32[]{:S(2)}) collective-permute-start(bf16[1,32,768]{2,1,0:T(8,128)(2,1)S(1)} %get-tuple-element.32), channel_id=1, source_target_pairs={{0,256},{256,0},{1,257},{257,1},{2,258},{258,2},{3,259},{259,3},{4... | collective-permute-start | bytes 147464 | tf_op jit(solution)/shard_map/ppermute | solution.py:295
  96.0 2.1 %collective-permute-done.5.refs_1_ = bf16[1,32,768]{2,1,0:T(8,128)(2,1)S(1)} collective-permute-done((bf16[1,32,768]{2,1,0:T(8,128)(2,1)S(1)}, bf16[1,32,768]{2,1,0:T(8,128)(2,1)S(1)}, u32[]{:S(2)}, u32[]{:S(2)}) %collective-permute-start.5) | collective-permute-done | bytes 49184 | tf_op jit(solution)/shard_map/ppermute | solution.py:295
  98.0 0.6 shard_map.109
  98.7 0.0 all-to-all-done.1.back_ref
  98.7 0.0 copy-done.1
  98.7 1.3 %shard_map.105 = bf16[4,64,1024]{2,1,0:T(8,128)(2,1)} custom-call(bf16[4,64,64]{2,1,0:T(8,128)(2,1)S(1)} %copy-done.1, bf16[16,32,1024]{2,1,0:T(8,128)(2,1)S(1)} %all-to-all-done.1.back_ref), custom_call_target="tpu_custom_call" | custom-call | flops 134217728 | bytes 4194304 | tf_op jit(solution)/shard_map/pallas_call | solution.py:314
  (1 shorter events, 0.0 us)
Async XLA Ops:
  0.6 44.0 %copy-start.3 = (bf16[256,1024]{1,0:T(8,128)(2,1)S(1)}, bf16[256,1024]{1,0:T(8,128)(2,1)}, u32[]{:S(2)}) copy-start(bf16[256,1024]{1,0:T(8,128)(2,1)} %down_w_ref.1) | copy-start | bytes 1572868
  3.0 41.7 %copy-start.2 = (bf16[4,128,1024]{2,1,0:T(8,128)(2,1)S(1)}, bf16[4,128,1024]{2,1,0:T(8,128)(2,1)}, u32[]{:S(2)}) copy-start(bf16[4,128,1024]{2,1,0:T(8,128)(2,1)} %x_ref.1) | copy-start | bytes 3145732
  3.0 41.6 %copy-start.4 = (bf16[1024,256]{1,0:T(8,128)(2,1)S(1)}, bf16[1024,256]{1,0:T(8,128)(2,1)}, u32[]{:S(2)}) copy-start(bf16[1024,256]{1,0:T(8,128)(2,1)} %gate_w_ref.3) | copy-start | bytes 1572868
  3.0 41.6 %copy-start.5 = (bf16[1024,256]{1,0:T(8,128)(2,1)S(1)}, bf16[1024,256]{1,0:T(8,128)(2,1)}, u32[]{:S(2)}) copy-start(bf16[1024,256]{1,0:T(8,128)(2,1)} %up_w_ref.3) | copy-start | bytes 1572868
  49.5 1.0 copy-start
  50.5 48.2 %all-to-all-start.1 = ((bf16[16,32,1024]{2,1,0:T(8,128)(2,1)}), bf16[16,32,1024]{2,1,0:T(8,128)(2,1)S(1)}, u32[]{:S(2)}, u32[]{:S(2)}) async-start(bf16[16,32,1024]{2,1,0:T(8,128)(2,1)} %copy-done), calls=%async_computation.1 | async-start | bytes 2097152 | tf_op jit(solution)/shard_map/all_to_all | solution.py:292
  54.0 4.2 %collective-permute-start = (bf16[16,32,768]{2,1,0:T(8,128)(2,1)S(1)}, bf16[16,32,768]{2,1,0:T(8,128)(2,1)S(1)}, u32[]{:S(2)}, u32[]{:S(2)}) collective-permute-start(bf16[16,32,768]{2,1,0:T(8,128)(2,1)S(1)} %get-tuple-element.24), channel_id=1, source_target_pairs={{0,16},{16,0},{1,17},{17,1},{2,18},{18,2},{3,19},{19,3},{4,20},{20... | collective-permute-start | bytes 2359304 | tf_op jit(solution)/shard_map/ppermute | solution.py:295
  58.2 40.4 %copy-start.1 = (bf16[4,64,64]{2,1,0:T(8,128)(2,1)S(1)}, bf16[4,64,64]{2,1,0:T(8,128)(2,1)}, u32[]{:S(2)}) copy-start(bf16[4,64,64]{2,1,0:T(8,128)(2,1)} %get-tuple-element.20.pick_ref) | copy-start | bytes 98308
  58.4 13.1 %collective-permute-start.1 = (bf16[8,32,768]{2,1,0:T(8,128)(2,1)S(1)}, bf16[8,32,768]{2,1,0:T(8,128)(2,1)S(1)}, u32[]{:S(2)}, u32[]{:S(2)}) collective-permute-start(bf16[8,32,768]{2,1,0:T(8,128)(2,1)S(1)} %get-tuple-element.26), channel_id=1, source_target_pairs={{0,32},{32,0},{64,96},{96,64},{128,160},{160,128},{192,224},{224,1... | collective-permute-start | bytes 1179656 | tf_op jit(solution)/shard_map/ppermute | solution.py:295
  71.5 14.4 %collective-permute-start.2 = (bf16[2,32,768]{2,1,0:T(8,128)(2,1)S(1)}, bf16[2,32,768]{2,1,0:T(8,128)(2,1)S(1)}, u32[]{:S(2)}, u32[]{:S(2)}) collective-permute-start(bf16[2,32,768]{2,1,0:T(8,128)(2,1)S(1)} %get-tuple-element.28), channel_id=1, source_target_pairs={{0,160},{32,128},{64,224},{96,192},{128,32},{160,0},{192,96},{224,... | collective-permute-start | bytes 294920 | tf_op jit(solution)/shard_map/ppermute | solution.py:295
  75.4 10.5 %collective-permute-start.3 = (bf16[2,32,768]{2,1,0:T(8,128)(2,1)S(1)}, bf16[2,32,768]{2,1,0:T(8,128)(2,1)S(1)}, u32[]{:S(2)}, u32[]{:S(2)}) collective-permute-start(bf16[2,32,768]{2,1,0:T(8,128)(2,1)S(1)} %get-tuple-element.29), channel_id=1, source_target_pairs={{0,64},{32,96},{64,128},{96,160},{128,192},{160,224},{192,0},{224,... | collective-permute-start | bytes 294920 | tf_op jit(solution)/shard_map/ppermute | solution.py:295
  80.2 10.3 %collective-permute-start.4 = (bf16[2,32,768]{2,1,0:T(8,128)(2,1)S(1)}, bf16[2,32,768]{2,1,0:T(8,128)(2,1)S(1)}, u32[]{:S(2)}, u32[]{:S(2)}) collective-permute-start(bf16[2,32,768]{2,1,0:T(8,128)(2,1)S(1)} %get-tuple-element.30), channel_id=1, source_target_pairs={{0,192},{32,224},{64,0},{96,32},{128,64},{160,96},{192,128},{224,1... | collective-permute-start | bytes 294920 | tf_op jit(solution)/shard_map/ppermute | solution.py:295
  90.6 7.4 %collective-permute-start.5 = (bf16[1,32,768]{2,1,0:T(8,128)(2,1)S(1)}, bf16[1,32,768]{2,1,0:T(8,128)(2,1)S(1)}, u32[]{:S(2)}, u32[]{:S(2)}) collective-permute-start(bf16[1,32,768]{2,1,0:T(8,128)(2,1)S(1)} %get-tuple-element.32), channel_id=1, source_target_pairs={{0,256},{256,0},{1,257},{257,1},{2,258},{258,2},{3,259},{259,3},{4... | collective-permute-start | bytes 147464 | tf_op jit(solution)/shard_map/ppermute | solution.py:295

commit v6 on v5

--- a/solution.py
+++ b/solution.py
@@ -138,15 +138,20 @@
         got_all_ref[m * slots : (m + 1) * slots] = got_ref[
             :, m * CAPS : (m + 1) * CAPS, :
         ].reshape(slots, width)
-    gate = dot(x, gate_w_ref[...], (1, 0))
-    up = dot(x, up_w_ref[...], (1, 0))
-    sigmoid = jax.nn.sigmoid(gate)
-    activated = gate * sigmoid
-    hidden = (activated * up).astype(jnp.bfloat16)
-    to_gate = up * sigmoid * (1.0 + gate * (1.0 - sigmoid))
-    d_hidden = dot(got_all_ref[...], down_w_ref[...], (1, 1))
-    d_both_ref[:, :cols] = (d_hidden * to_gate).astype(jnp.bfloat16)
-    d_both_ref[:, cols:] = (d_hidden * activated).astype(jnp.bfloat16)
+    hidden = []
+    half = micro * slots // 2
+    for start in (0, half):
+        span = slice(start, start + half)
+        gate = dot(x[span], gate_w_ref[...], (1, 0))
+        up = dot(x[span], up_w_ref[...], (1, 0))
+        d_hidden = dot(got_all_ref[span], down_w_ref[...], (1, 1))
+        sigmoid = jax.nn.sigmoid(gate)
+        activated = gate * sigmoid
+        hidden.append((activated * up).astype(jnp.bfloat16))
+        to_gate = up * sigmoid * (1.0 + gate * (1.0 - sigmoid))
+        d_both_ref[span, :cols] = (d_hidden * to_gate).astype(jnp.bfloat16)
+        d_both_ref[span, cols:] = (d_hidden * activated).astype(jnp.bfloat16)
+    hidden = jnp.concatenate(hidden, axis=0)
     total = dot(x, d_both_ref[...], (0, 0))
     all_ref[:, :, : 2 * cols] = total.reshape(pieces, rows, 2 * cols)
     total = dot(got_all_ref[...], hidden, (0, 0))

time: 100 us -> 99.9 us (level)
  no operation moved by 1% of the time
where the time goes in v6:
time: 99.9 us; the launch traced here: 99.5 us
  blocking collectives  41.6 us (42%)
  starting transfers between devices  24.1 us (24%)
  waiting for transfers between devices  23.1 us (23%)
  Pallas kernels  8.84 us (9%)
  local copies, waits for them, and re-layouts  1 us (1%)
    all_to_all x1, blocking collectives, per_device(): got = lax.all_to_all(send, EXPERT, 0, 0, tiled=True)  41.6 us
    ppermute x6, waiting for transfers between devices, swap(): lax.ppermute(value, axis, [(i, partner(i)) for i in range(lax.axis_size(a...  23.1 us
    ppermute x6, starting transfers between devices, swap(): lax.ppermute(value, axis, [(i, partner(i)) for i in range(lax.axis_size(a...  20.5 us
    all_to_all x1, starting transfers between devices, per_device(): back = lax.all_to_all(back_send, EXPERT, 0, 0, tiled=True)  3.55 us
    pallas_call x1, Pallas kernels, per_device(): call(route_body, (shape((holders, micro * CAPS, width), bf16), shape((mic...  2.37 us
    pallas_call x1, Pallas kernels, per_device(): call(weight_body, (shape((micro * slots, 2 * cols), bf16), shape(lot(piec...  2.21 us
    pallas_call x1, Pallas kernels, per_device(): call(slot_body, (shape((holders, micro * CAPS, width), bf16),), 1 << 30,...  2.13 us
  transfers between devices with their start and end apart: 7, of which 5 were waited for; matrix products, arithmetic and copies ran while one was open for 0% of the time, Pallas kernels for 1%

profile of v6, /device:TPU:50, one launch (start us, length us, event | category | flops | bytes accessed | tf_op | source)
XLA Modules:
  0.0 99.5 jit_solution(11404135025988382599)
XLA Ops:
  0.6 0.0 copy-start.3
  0.6 2.4 %shard_map.102 = (bf16[16,32,1024]{2,1,0:T(8,128)(2,1)}, bf16[4,64,64]{2,1,0:T(8,128)(2,1)}) custom-call(s32[4,8,64]{2,1,0:T(8,128)} %bitcast.2, bf16[4,8,64]{2,1,0:T(8,128)(2,1)} %bitcast.3, bf16[4,64,1024]{2,1,0:T(8,128)(2,1)} %grad_hbm.1), custom_call_target="tpu_custom_call" | custom-call | flops 134217728 | bytes 4194304 | tf_op jit(solution)/shard_map/pallas_call | solution.py:250
  3.0 0.0 copy-start.2
  3.0 0.0 copy-start.4
  3.0 0.0 copy-start.5
  3.1 41.6 %all_to_all.10.got_ref = bf16[16,32,1024]{2,1,0:T(8,128)(2,1)S(1)} all-to-all(bf16[16,32,1024]{2,1,0:T(8,128)(2,1)} %get-tuple-element.21), channel_id=1, replica_groups=mesh['zl'=2,'y'=8,'core'=2,'x'=4,'zq'=2,'zp'=2] {'x','zq','zp'}, dimensions={0} | all-to-all | bytes 2097152 | tf_op jit(solution)/shard_map/all_to_all | solution.py:270
  44.7 0.0 copy-done.3
  44.7 0.0 copy-done.2
  44.7 0.0 copy-done.4
  44.7 0.0 copy-done.5
  44.7 2.2 %shard_map.103 = (bf16[512,512]{1,0:T(8,128)(2,1)S(1)}, f32[16,32,768]{2,1,0:T(8,128)S(1)}, bf16[16,32,768]{2,1,0:T(8,128)(2,1)S(1)}) custom-call(bf16[16,32,1024]{2,1,0:T(8,128)(2,1)S(1)} %all_to_all.10.got_ref, bf16[4,128,1024]{2,1,0:T(8,128)(2,1)S(1)} %copy-done.2, bf16[1024,256]{1,0:T(8,128)(2,1)S(1)} %copy-done.4, bf16[1024,256]{1,0:T(8,128)(2,1)S(1)} %copy-done.5, ...), custom_call_target="tpu_custom_call" | custom-call | flops 2147483648 | bytes 4194304 | tf_op jit(solution)/shard_map/pallas_call | solution.py:275
  46.9 2.1 %shard_map.104 = bf16[16,32,1024]{2,1,0:T(8,128)(2,1)S(1)} custom-call(bf16[512,512]{1,0:T(8,128)(2,1)S(1)} %get-tuple-element.22.d_both_ref, bf16[1024,256]{1,0:T(8,128)(2,1)S(1)} %copy-done.4, bf16[1024,256]{1,0:T(8,128)(2,1)S(1)} %copy-done.5), custom_call_target="tpu_custom_call" | custom-call | flops 1073741824 | bytes 4194304 | tf_op jit(solution)/shard_map/pallas_call | solution.py:286
  49.0 0.0 copy-start
  49.1 1.0 copy-done
  50.0 3.5 %all-to-all-start.1 = ((bf16[16,32,1024]{2,1,0:T(8,128)(2,1)}), bf16[16,32,1024]{2,1,0:T(8,128)(2,1)S(1)}, u32[]{:S(2)}, u32[]{:S(2)}) async-start(bf16[16,32,1024]{2,1,0:T(8,128)(2,1)} %copy-done), calls=%async_computation.1 | async-start | bytes 2097152 | tf_op jit(solution)/shard_map/all_to_all | solution.py:297
  53.6 1.9 %collective-permute-start = (bf16[16,32,768]{2,1,0:T(8,128)(2,1)S(1)}, bf16[16,32,768]{2,1,0:T(8,128)(2,1)S(1)}, u32[]{:S(2)}, u32[]{:S(2)}) collective-permute-start(bf16[16,32,768]{2,1,0:T(8,128)(2,1)S(1)} %get-tuple-element.24), channel_id=1, source_target_pairs={{0,16},{16,0},{1,17},{17,1},{2,18},{18,2},{3,19},{19,3},{4,20},{20... | collective-permute-start | bytes 2359304 | tf_op jit(solution)/shard_map/ppermute | solution.py:300
  55.5 2.3 %collective-permute-done.other_ref = bf16[16,32,768]{2,1,0:T(8,128)(2,1)S(1)} collective-permute-done((bf16[16,32,768]{2,1,0:T(8,128)(2,1)S(1)}, bf16[16,32,768]{2,1,0:T(8,128)(2,1)S(1)}, u32[]{:S(2)}, u32[]{:S(2)}) %collective-permute-start) | collective-permute-done | bytes 786464 | tf_op jit(solution)/shard_map/ppermute | solution.py:300
  57.8 0.0 copy-start.1
  57.8 0.1 shard_map.106
  57.9 2.6 %collective-permute-start.1 = (bf16[8,32,768]{2,1,0:T(8,128)(2,1)S(1)}, bf16[8,32,768]{2,1,0:T(8,128)(2,1)S(1)}, u32[]{:S(2)}, u32[]{:S(2)}) collective-permute-start(bf16[8,32,768]{2,1,0:T(8,128)(2,1)S(1)} %get-tuple-element.26), channel_id=1, source_target_pairs={{0,32},{32,0},{64,96},{96,64},{128,160},{160,128},{192,224},{224,1... | collective-permute-start | bytes 1179656 | tf_op jit(solution)/shard_map/ppermute | solution.py:300
  60.5 10.5 %collective-permute-done.1.other_ref = bf16[8,32,768]{2,1,0:T(8,128)(2,1)S(1)} collective-permute-done((bf16[8,32,768]{2,1,0:T(8,128)(2,1)S(1)}, bf16[8,32,768]{2,1,0:T(8,128)(2,1)S(1)}, u32[]{:S(2)}, u32[]{:S(2)}) %collective-permute-start.1) | collective-permute-done | bytes 393248 | tf_op jit(solution)/shard_map/ppermute | solution.py:300
  70.9 0.1 shard_map.107
  71.0 3.9 %collective-permute-start.2 = (bf16[2,32,768]{2,1,0:T(8,128)(2,1)S(1)}, bf16[2,32,768]{2,1,0:T(8,128)(2,1)S(1)}, u32[]{:S(2)}, u32[]{:S(2)}) collective-permute-start(bf16[2,32,768]{2,1,0:T(8,128)(2,1)S(1)} %get-tuple-element.28), channel_id=1, source_target_pairs={{0,160},{32,128},{64,224},{96,192},{128,32},{160,0},{192,96},{224,... | collective-permute-start | bytes 294920 | tf_op jit(solution)/shard_map/ppermute | solution.py:300
  74.9 4.8 %collective-permute-start.3 = (bf16[2,32,768]{2,1,0:T(8,128)(2,1)S(1)}, bf16[2,32,768]{2,1,0:T(8,128)(2,1)S(1)}, u32[]{:S(2)}, u32[]{:S(2)}) collective-permute-start(bf16[2,32,768]{2,1,0:T(8,128)(2,1)S(1)} %get-tuple-element.29), channel_id=1, source_target_pairs={{0,64},{32,96},{64,128},{96,160},{128,192},{160,224},{192,0},{224,... | collective-permute-start | bytes 294920 | tf_op jit(solution)/shard_map/ppermute | solution.py:300
  79.8 1.9 %collective-permute-start.4 = (bf16[2,32,768]{2,1,0:T(8,128)(2,1)S(1)}, bf16[2,32,768]{2,1,0:T(8,128)(2,1)S(1)}, u32[]{:S(2)}, u32[]{:S(2)}) collective-permute-start(bf16[2,32,768]{2,1,0:T(8,128)(2,1)S(1)} %get-tuple-element.30), channel_id=1, source_target_pairs={{0,192},{32,224},{64,0},{96,32},{128,64},{160,96},{192,128},{224,1... | collective-permute-start | bytes 294920 | tf_op jit(solution)/shard_map/ppermute | solution.py:300
  81.7 3.7 %collective-permute-done.2.refs_0_ = bf16[2,32,768]{2,1,0:T(8,128)(2,1)S(1)} collective-permute-done((bf16[2,32,768]{2,1,0:T(8,128)(2,1)S(1)}, bf16[2,32,768]{2,1,0:T(8,128)(2,1)S(1)}, u32[]{:S(2)}, u32[]{:S(2)}) %collective-permute-start.2) | collective-permute-done | bytes 98336 | tf_op jit(solution)/shard_map/ppermute | solution.py:300
  85.4 0.0 collective-permute-done.3.refs_1_
  85.4 4.7 %collective-permute-done.4.refs_2_ = bf16[2,32,768]{2,1,0:T(8,128)(2,1)S(1)} collective-permute-done((bf16[2,32,768]{2,1,0:T(8,128)(2,1)S(1)}, bf16[2,32,768]{2,1,0:T(8,128)(2,1)S(1)}, u32[]{:S(2)}, u32[]{:S(2)}) %collective-permute-start.4) | collective-permute-done | bytes 98336 | tf_op jit(solution)/shard_map/ppermute | solution.py:300
  90.1 5.4 %collective-permute-start.5 = (bf16[1,32,768]{2,1,0:T(8,128)(2,1)S(1)}, bf16[1,32,768]{2,1,0:T(8,128)(2,1)S(1)}, u32[]{:S(2)}, u32[]{:S(2)}) collective-permute-start(bf16[1,32,768]{2,1,0:T(8,128)(2,1)S(1)} %get-tuple-element.32), channel_id=1, source_target_pairs={{0,256},{256,0},{1,257},{257,1},{2,258},{258,2},{3,259},{259,3},{4... | collective-permute-start | bytes 147464 | tf_op jit(solution)/shard_map/ppermute | solution.py:300
  95.5 2.1 %collective-permute-done.5.refs_1_ = bf16[1,32,768]{2,1,0:T(8,128)(2,1)S(1)} collective-permute-done((bf16[1,32,768]{2,1,0:T(8,128)(2,1)S(1)}, bf16[1,32,768]{2,1,0:T(8,128)(2,1)S(1)}, u32[]{:S(2)}, u32[]{:S(2)}) %collective-permute-start.5) | collective-permute-done | bytes 49184 | tf_op jit(solution)/shard_map/ppermute | solution.py:300
  97.5 0.6 shard_map.109
  98.2 0.0 all-to-all-done.1.back_ref
  98.2 0.0 copy-done.1
  98.2 1.3 %shard_map.105 = bf16[4,64,1024]{2,1,0:T(8,128)(2,1)} custom-call(bf16[4,64,64]{2,1,0:T(8,128)(2,1)S(1)} %copy-done.1, bf16[16,32,1024]{2,1,0:T(8,128)(2,1)S(1)} %all-to-all-done.1.back_ref), custom_call_target="tpu_custom_call" | custom-call | flops 134217728 | bytes 4194304 | tf_op jit(solution)/shard_map/pallas_call | solution.py:319
  (1 shorter events, 0.0 us)
Async XLA Ops:
  0.6 44.0 %copy-start.3 = (bf16[256,1024]{1,0:T(8,128)(2,1)S(1)}, bf16[256,1024]{1,0:T(8,128)(2,1)}, u32[]{:S(2)}) copy-start(bf16[256,1024]{1,0:T(8,128)(2,1)} %down_w_ref.1) | copy-start | bytes 1572868
  3.0 41.7 %copy-start.2 = (bf16[4,128,1024]{2,1,0:T(8,128)(2,1)S(1)}, bf16[4,128,1024]{2,1,0:T(8,128)(2,1)}, u32[]{:S(2)}) copy-start(bf16[4,128,1024]{2,1,0:T(8,128)(2,1)} %x_ref.1) | copy-start | bytes 3145732
  3.0 41.6 %copy-start.4 = (bf16[1024,256]{1,0:T(8,128)(2,1)S(1)}, bf16[1024,256]{1,0:T(8,128)(2,1)}, u32[]{:S(2)}) copy-start(bf16[1024,256]{1,0:T(8,128)(2,1)} %gate_w_ref.3) | copy-start | bytes 1572868
  3.0 41.6 %copy-start.5 = (bf16[1024,256]{1,0:T(8,128)(2,1)S(1)}, bf16[1024,256]{1,0:T(8,128)(2,1)}, u32[]{:S(2)}) copy-start(bf16[1024,256]{1,0:T(8,128)(2,1)} %up_w_ref.3) | copy-start | bytes 1572868
  49.0 1.0 copy-start
  50.0 48.2 %all-to-all-start.1 = ((bf16[16,32,1024]{2,1,0:T(8,128)(2,1)}), bf16[16,32,1024]{2,1,0:T(8,128)(2,1)S(1)}, u32[]{:S(2)}, u32[]{:S(2)}) async-start(bf16[16,32,1024]{2,1,0:T(8,128)(2,1)} %copy-done), calls=%async_computation.1 | async-start | bytes 2097152 | tf_op jit(solution)/shard_map/all_to_all | solution.py:297
  53.6 4.2 %collective-permute-start = (bf16[16,32,768]{2,1,0:T(8,128)(2,1)S(1)}, bf16[16,32,768]{2,1,0:T(8,128)(2,1)S(1)}, u32[]{:S(2)}, u32[]{:S(2)}) collective-permute-start(bf16[16,32,768]{2,1,0:T(8,128)(2,1)S(1)} %get-tuple-element.24), channel_id=1, source_target_pairs={{0,16},{16,0},{1,17},{17,1},{2,18},{18,2},{3,19},{19,3},{4,20},{20... | collective-permute-start | bytes 2359304 | tf_op jit(solution)/shard_map/ppermute | solution.py:300
  57.8 40.4 %copy-start.1 = (bf16[4,64,64]{2,1,0:T(8,128)(2,1)S(1)}, bf16[4,64,64]{2,1,0:T(8,128)(2,1)}, u32[]{:S(2)}) copy-start(bf16[4,64,64]{2,1,0:T(8,128)(2,1)} %get-tuple-element.20.pick_ref) | copy-start | bytes 98308
  57.9 13.1 %collective-permute-start.1 = (bf16[8,32,768]{2,1,0:T(8,128)(2,1)S(1)}, bf16[8,32,768]{2,1,0:T(8,128)(2,1)S(1)}, u32[]{:S(2)}, u32[]{:S(2)}) collective-permute-start(bf16[8,32,768]{2,1,0:T(8,128)(2,1)S(1)} %get-tuple-element.26), channel_id=1, source_target_pairs={{0,32},{32,0},{64,96},{96,64},{128,160},{160,128},{192,224},{224,1... | collective-permute-start | bytes 1179656 | tf_op jit(solution)/shard_map/ppermute | solution.py:300
  71.0 14.4 %collective-permute-start.2 = (bf16[2,32,768]{2,1,0:T(8,128)(2,1)S(1)}, bf16[2,32,768]{2,1,0:T(8,128)(2,1)S(1)}, u32[]{:S(2)}, u32[]{:S(2)}) collective-permute-start(bf16[2,32,768]{2,1,0:T(8,128)(2,1)S(1)} %get-tuple-element.28), channel_id=1, source_target_pairs={{0,160},{32,128},{64,224},{96,192},{128,32},{160,0},{192,96},{224,... | collective-permute-start | bytes 294920 | tf_op jit(solution)/shard_map/ppermute | solution.py:300
  74.9 10.5 %collective-permute-start.3 = (bf16[2,32,768]{2,1,0:T(8,128)(2,1)S(1)}, bf16[2,32,768]{2,1,0:T(8,128)(2,1)S(1)}, u32[]{:S(2)}, u32[]{:S(2)}) collective-permute-start(bf16[2,32,768]{2,1,0:T(8,128)(2,1)S(1)} %get-tuple-element.29), channel_id=1, source_target_pairs={{0,64},{32,96},{64,128},{96,160},{128,192},{160,224},{192,0},{224,... | collective-permute-start | bytes 294920 | tf_op jit(solution)/shard_map/ppermute | solution.py:300
  79.8 10.3 %collective-permute-start.4 = (bf16[2,32,768]{2,1,0:T(8,128)(2,1)S(1)}, bf16[2,32,768]{2,1,0:T(8,128)(2,1)S(1)}, u32[]{:S(2)}, u32[]{:S(2)}) collective-permute-start(bf16[2,32,768]{2,1,0:T(8,128)(2,1)S(1)} %get-tuple-element.30), channel_id=1, source_target_pairs={{0,192},{32,224},{64,0},{96,32},{128,64},{160,96},{192,128},{224,1... | collective-permute-start | bytes 294920 | tf_op jit(solution)/shard_map/ppermute | solution.py:300
  90.1 7.4 %collective-permute-start.5 = (bf16[1,32,768]{2,1,0:T(8,128)(2,1)S(1)}, bf16[1,32,768]{2,1,0:T(8,128)(2,1)S(1)}, u32[]{:S(2)}, u32[]{:S(2)}) collective-permute-start(bf16[1,32,768]{2,1,0:T(8,128)(2,1)S(1)} %get-tuple-element.32), channel_id=1, source_target_pairs={{0,256},{256,0},{1,257},{257,1},{2,258},{258,2},{3,259},{259,3},{4... | collective-permute-start | bytes 147464 | tf_op jit(solution)/shard_map/ppermute | solution.py:300
